TPU v7x, 32 devices: a whole 2x2x4 slice. The times are simulated.
32 devices in a mesh: slab: 8 (over y, x, core), det: 4 (over z).
Axes of the slice: x: 2, y: 2, z: 4, core: 2. Of those that a mesh axis runs over, the one named last changes fastest.
Arguments:
- traces: float32 [32, 128, 4096], P(('slab', 'det')), may hold values from -6 to 6
- tables: bfloat16 [32, 256, 2048], P('slab', None, 'det'), may hold values from -0.0625 to 0.0625
- slab_range: int32 [32, 2], P(('slab', 'det')), may hold values from 0 to 7, as said below
- table_slot: int32 [32, 7], P(('slab', 'det')), may hold values from 0 to 3
- sample_start: int32 [32, 7], P(('slab', 'det')), may hold values from 0 to 3840
Outputs:
- image: float32 [128, 16384], P(None, ('slab', 'det'))
Inputs may be any that keep to these rules, and one draw needn't show every extreme that they name: For detector d with home slab g = d // 4: max(0, g - 3) <= slab_range[d, 0] <= g <= slab_range[d, 1] <= min(7, g + 3); some detectors reach the full 3 on both sides where the grid allows.
All inputs are finite; a program needn't handle non-finite values.
Results may differ from a plain program's by a relative error of at most 0.007.
Values may be sent and summed in bfloat16 or wider, within the bound.
No kernel may reach another device: no remote copies, remote signals or barrier semaphores. Data moves between devices by JAX's collectives and lax.ppermute only.
A program may use at most 64 MiB of HBM per device.

v0:
```python
import jax
import jax.numpy as jnp
from jax import lax
from jax.sharding import PartitionSpec as P

KWIN = 256
NTAB = 4
RANGE = 3


def shifted(x, axis, by):
    peers = lax.axis_size(axis)
    pairs = [(i, i + by) for i in range(peers) if 0 <= i + by < peers]
    return lax.ppermute(x, axis, pairs)


def cut_windows(trace_rows, starts):

    def single(trace_row, first_index):
        return lax.dynamic_slice_in_dim(trace_row, first_index, KWIN, 1)

    return jax.vmap(single)(trace_rows, starts)


def bin_windows(windows, slot_ids, active):
    onehot = (slot_ids[:, None] == jnp.arange(NTAB, dtype=jnp.int32)[None, :]) & active[:, None]
    onehot = onehot.astype(jnp.bfloat16)
    return jnp.einsum("it,ifk->tfk", onehot, windows, preferred_element_type=jnp.float32)


def body(traces, tables, slab_range, table_slot, sample_start):
    position = lax.axis_index("slab")
    samples = traces.astype(jnp.bfloat16)
    own_active = (slab_range[:, 0] <= position) & (position <= slab_range[:, 1])
    stacked = bin_windows(
        cut_windows(samples, sample_start[:, RANGE]), table_slot[:, RANGE], own_active
    )
    for offset in list(range(-RANGE, 0)) + list(range(1, RANGE + 1)):
        target = position + offset
        active = (slab_range[:, 0] <= target) & (target <= slab_range[:, 1])
        windows = cut_windows(samples, sample_start[:, offset + RANGE])
        windows = windows * active[:, None, None].astype(jnp.bfloat16)
        arrived_windows, arrived_slots = shifted(
            (windows, table_slot[:, offset + RANGE]), "slab", offset
        )
        everything = jnp.ones(arrived_slots.shape, jnp.bool_)
        stacked = stacked + bin_windows(arrived_windows, arrived_slots, everything)
    binned = stacked.astype(jnp.bfloat16)
    partial_image = jnp.einsum(
        "tfk,tkv->fv",
        binned,
        lax.all_gather(tables, "det", axis=2, tiled=True),
        preferred_element_type=jnp.float32,
    )
    return lax.psum_scatter(partial_image, "det", scatter_dimension=1, tiled=True)


def solution(mesh):
    placed = (
        P(("slab", "det"), None, None),
        P("slab", None, "det"),
        P(("slab", "det"), None),
        P(("slab", "det"), None),
        P(("slab", "det"), None),
    )
    return jax.shard_map(
        body, mesh=mesh, in_specs=placed, out_specs=P(None, ("slab", "det")), check_vma=False
    )
```

profile of v0, /device:TPU:0, one launch (start us, length us, event | category | flops | bytes accessed | tf_op | source)
XLA Modules:
  0.0 129.3 jit_solution(1520195266104620349)
XLA Ops:
  6.5 0.7 all-gather.2.cloned.1.call-update
  7.3 1.6 %fusion.21 = (s32[1,1]{1,0:T(1,128)}, s32[1,1]{1,0:T(1,128)}, s32[1,1]{1,0:T(1,128)}, s32[1,1]{1,0:T(1,128)}, s32[1,1]{1,0:T(1,128)}, /*index=5*/s32[1,1]{1,0:T(1,128)}, s32[1,1]{1,0:T(1,128)}) fusion(s32[1,7]{1,0:T(1,128)} %param.8), kind=kLoop, calls=%fused_computation.43 | loop fusion | bytes 56 | tf_op jit(solution)/shard_map/slice | solution.py:36
  8.9 3.0 %collective-permute-start.6 = (s32[1]{0:T(128)}, s32[1]{0:T(128)}, u32[]{:S(2)}, u32[]{:S(2)}) collective-permute-start(s32[1]{0:T(128)} %bitcast.33), channel_id=1, source_target_pairs={{0,4},{4,8},{8,12},{12,16},{16,20},{20,24},{24,28},{1,5},{5,9},{9,... | collective-permute-start | bytes 20 | tf_op jit(solution)/shard_map/ppermute | solution.py:14
  11.9 1.3 collective-permute-start.4
  13.1 1.3 collective-permute-start.2
  14.4 1.3 collective-permute-start
  15.7 7.7 %collective-permute-start.10 = (s32[1]{0:T(128)}, s32[1]{0:T(128)}, u32[]{:S(2)}, u32[]{:S(2)}) collective-permute-start(s32[1]{0:T(128)} %bitcast.49), channel_id=1, source_target_pairs={{0,12},{4,16},{8,20},{12,24},{16,28},{1,13},{5,17},{9,21},{13,25},... | collective-permute-start | bytes 20 | tf_op jit(solution)/shard_map/ppermute | solution.py:14
  23.4 1.3 %fusion.23 = (s32[1,1]{1,0:T(1,128)}, s32[1,1]{1,0:T(1,128)}) fusion(s32[1,2]{1,0:T(1,128)} %param.7), kind=kLoop, calls=%fused_computation.45 | loop fusion | bytes 16 | tf_op jit(solution)/shard_map/slice | solution.py:34
  33.7 1.6 %fusion.22 = (s32[1,1]{1,0:T(1,128)}, s32[1,1]{1,0:T(1,128)}, s32[1,1]{1,0:T(1,128)}, s32[1,1]{1,0:T(1,128)}, s32[1,1]{1,0:T(1,128)}, /*index=5*/s32[1,1]{1,0:T(1,128)}, s32[1,1]{1,0:T(1,128)}) fusion(s32[1,7]{1,0:T(1,128)} %param.9), kind=kLoop, calls=%fused_computation.44 | loop fusion | bytes 56 | tf_op jit(solution)/shard_map/slice | solution.py:36
  44.2 1.7 %convert_element_type.10 = bf16[1,128,4096]{2,1,0:T(8,128)(2,1)S(1)} convert(f32[1,128,4096]{2,1,0:T(8,128)} %param.5) | non-fusion elementwise | flops 524288 | bytes 3145728 | tf_op jit(solution)/shard_map/convert_element_type | solution.py:33
  51.2 5.9 %collective-permute-start.8 = (s32[1]{0:T(128)}, s32[1]{0:T(128)}, u32[]{:S(2)}, u32[]{:S(2)}) collective-permute-start(s32[1]{0:T(128)} %bitcast.41), channel_id=1, source_target_pairs={{0,8},{4,12},{8,16},{12,20},{16,24},{20,28},{1,9},{5,13},{9,17},{1... | collective-permute-start | bytes 20 | tf_op jit(solution)/shard_map/ppermute | solution.py:14
  57.1 0.7 fusion.18
  57.8 1.3 %collective-permute-start.11 = (bf16[1,128,256]{2,1,0:T(8,128)(2,1)S(1)}, bf16[1,128,256]{2,1,0:T(8,128)(2,1)S(1)}, u32[]{:S(2)}, u32[]{:S(2)}) collective-permute-start(bf16[1,128,256]{2,1,0:T(8,128)(2,1)S(1)} %get-tuple-element.83), channel_id=1, source_target_pairs={{0,12},{4,16},{8,20},{12,24},{16,28},{1,13},{5,17},{9,21},{13,25},... | collective-permute-start | bytes 196616 | tf_op jit(solution)/shard_map/ppermute | solution.py:14
  59.8 2.9 %collective-permute-start.9 = (bf16[1,128,256]{2,1,0:T(8,128)(2,1)S(1)}, bf16[1,128,256]{2,1,0:T(8,128)(2,1)S(1)}, u32[]{:S(2)}, u32[]{:S(2)}) collective-permute-start(bf16[1,128,256]{2,1,0:T(8,128)(2,1)S(1)} %get-tuple-element.84), channel_id=1, source_target_pairs={{0,8},{4,12},{8,16},{12,20},{16,24},{20,28},{1,9},{5,13},{9,17},{1... | collective-permute-start | bytes 196616 | tf_op jit(solution)/shard_map/ppermute | solution.py:14
  63.3 1.3 %collective-permute-start.7 = (bf16[1,128,256]{2,1,0:T(8,128)(2,1)S(1)}, bf16[1,128,256]{2,1,0:T(8,128)(2,1)S(1)}, u32[]{:S(2)}, u32[]{:S(2)}) collective-permute-start(bf16[1,128,256]{2,1,0:T(8,128)(2,1)S(1)} %get-tuple-element.85), channel_id=1, source_target_pairs={{0,4},{4,8},{8,12},{12,16},{16,20},{20,24},{24,28},{1,5},{5,9},{9,... | collective-permute-start | bytes 196616 | tf_op jit(solution)/shard_map/ppermute | solution.py:14
  65.2 1.3 collective-permute-start.5
  67.2 1.3 collective-permute-start.3
  68.5 0.7 fusion.19
  69.2 1.3 collective-permute-start.1
  70.6 4.5 %collective-permute-done.3 = bf16[1,128,256]{2,1,0:T(8,128)(2,1)S(1)} collective-permute-done((bf16[1,128,256]{2,1,0:T(8,128)(2,1)S(1)}, bf16[1,128,256]{2,1,0:T(8,128)(2,1)S(1)}, u32[]{:S(2)}, u32[]{:S(2)}) %collective-permute-start.3) | collective-permute-done | bytes 65568 | tf_op jit(solution)/shard_map/ppermute | solution.py:14
  75.1 1.9 %collective-permute-done.1 = bf16[1,128,256]{2,1,0:T(8,128)(2,1)S(1)} collective-permute-done((bf16[1,128,256]{2,1,0:T(8,128)(2,1)S(1)}, bf16[1,128,256]{2,1,0:T(8,128)(2,1)S(1)}, u32[]{:S(2)}, u32[]{:S(2)}) %collective-permute-start.1) | collective-permute-done | bytes 65568 | tf_op jit(solution)/shard_map/ppermute | solution.py:14
  77.0 15.4 %all-gather.2.cloned.1.call-done = bf16[4,256,2048]{2,1,0:T(8,128)(2,1)} async-done(((bf16[4,256,512]{2,1,0:T(8,128)(2,1)}), bf16[4,256,2048]{2,1,0:T(8,128)(2,1)}) %all-gather.2.cloned.1.call-update) | async-done | bytes 4194320 | tf_op jit(solution)/shard_map/all_gather | solution.py:52
  92.4 4.1 %convolution_bitcast_fusion = f32[128,2048]{1,0:T(8,128)} fusion(bf16[4,256,2048]{2,1,0:T(8,128)(2,1)} %all-gather.2.cloned.1.call-done, f32[128,256]{1,0:T(8,128)S(1)} %bitcast_convert_fusion, f32[4]{0:T(128)S(1)} %fusion.20, f32[128,256]{1,0:T(8,128)S(1)} %bitcast_convert_fusion.1, f32[4]{0:T(128)S(1)} %fusion.19, f32[128,256]{1,0:T(8,128)S(1)} %bitcast_convert_fusion.2, ...), kind=kOutput, calls=%fused_computation | convolution fusion | flops 538705920 | bytes 6160496 | tf_op jit(solution)/shard_map/tfk,tkv->fv/dot_general | solution.py:49
  96.5 25.9 %reduce-scatter.2.cloned.1.call-done = f32[128,512]{1,0:T(8,128)} async-done(((f32[128,2048]{1,0:T(8,128)}), f32[128,512]{1,0:T(8,128)}) %reduce-scatter.2.cloned.1.call-update) | async-done | bytes 262160 | tf_op jit(solution)/shard_map/reduce_scatter | solution.py:55
  (25 shorter events, 3.5 us)
Async XLA Ops:
  6.5 85.9 %all-gather.2.cloned.1.call-start = ((), (), s32[]{:S(2)}) async-start(), calls=%async_computation.1 | async-start | bytes 5242880 | tf_op jit(solution)/shard_map/all_gather | solution.py:52
  7.3 115.2 %reduce-scatter.2.cloned.1.call-start = ((), (), s32[]{:S(2)}) async-start(), calls=%async_computation.2 | async-start | bytes 1310720 | tf_op jit(solution)/shard_map/reduce_scatter | solution.py:55
  8.9 42.3 %collective-permute-start.6 = (s32[1]{0:T(128)}, s32[1]{0:T(128)}, u32[]{:S(2)}, u32[]{:S(2)}) collective-permute-start(s32[1]{0:T(128)} %bitcast.33), channel_id=1, source_target_pairs={{0,4},{4,8},{8,12},{12,16},{16,20},{20,24},{24,28},{1,5},{5,9},{9,... | collective-permute-start | bytes 20 | tf_op jit(solution)/shard_map/ppermute | solution.py:14
  11.9 46.0 %collective-permute-start.4 = (s32[1]{0:T(128)}, s32[1]{0:T(128)}, u32[]{:S(2)}, u32[]{:S(2)}) collective-permute-start(s32[1]{0:T(128)} %bitcast.25), channel_id=1, source_target_pairs={{4,0},{8,4},{12,8},{16,12},{20,16},{24,20},{28,24},{5,1},{9,5},{13... | collective-permute-start | bytes 20 | tf_op jit(solution)/shard_map/ppermute | solution.py:14
  13.1 46.6 %collective-permute-start.2 = (s32[1]{0:T(128)}, s32[1]{0:T(128)}, u32[]{:S(2)}, u32[]{:S(2)}) collective-permute-start(s32[1]{0:T(128)} %bitcast.17), channel_id=1, source_target_pairs={{8,0},{12,4},{16,8},{20,12},{24,16},{28,20},{9,1},{13,5},{17,9},{2... | collective-permute-start | bytes 20 | tf_op jit(solution)/shard_map/ppermute | solution.py:14
  14.4 48.8 %collective-permute-start = (s32[1]{0:T(128)}, s32[1]{0:T(128)}, u32[]{:S(2)}, u32[]{:S(2)}) collective-permute-start(s32[1]{0:T(128)} %bitcast.9), channel_id=1, source_target_pairs={{12,0},{16,4},{20,8},{24,12},{28,16},{13,1},{17,5},{21,9},{25,13},... | collective-permute-start | bytes 20 | tf_op jit(solution)/shard_map/ppermute | solution.py:14
  15.7 49.5 %collective-permute-start.10 = (s32[1]{0:T(128)}, s32[1]{0:T(128)}, u32[]{:S(2)}, u32[]{:S(2)}) collective-permute-start(s32[1]{0:T(128)} %bitcast.49), channel_id=1, source_target_pairs={{0,12},{4,16},{8,20},{12,24},{16,28},{1,13},{5,17},{9,21},{13,25},... | collective-permute-start | bytes 20 | tf_op jit(solution)/shard_map/ppermute | solution.py:14
  51.2 16.0 %collective-permute-start.8 = (s32[1]{0:T(128)}, s32[1]{0:T(128)}, u32[]{:S(2)}, u32[]{:S(2)}) collective-permute-start(s32[1]{0:T(128)} %bitcast.41), channel_id=1, source_target_pairs={{0,8},{4,12},{8,16},{12,20},{16,24},{20,28},{1,9},{5,13},{9,17},{1... | collective-permute-start | bytes 20 | tf_op jit(solution)/shard_map/ppermute | solution.py:14
  57.8 11.4 %collective-permute-start.11 = (bf16[1,128,256]{2,1,0:T(8,128)(2,1)S(1)}, bf16[1,128,256]{2,1,0:T(8,128)(2,1)S(1)}, u32[]{:S(2)}, u32[]{:S(2)}) collective-permute-start(bf16[1,128,256]{2,1,0:T(8,128)(2,1)S(1)} %get-tuple-element.83), channel_id=1, source_target_pairs={{0,12},{4,16},{8,20},{12,24},{16,28},{1,13},{5,17},{9,21},{13,25},... | collective-permute-start | bytes 196616 | tf_op jit(solution)/shard_map/ppermute | solution.py:14
  59.8 10.7 %collective-permute-start.9 = (bf16[1,128,256]{2,1,0:T(8,128)(2,1)S(1)}, bf16[1,128,256]{2,1,0:T(8,128)(2,1)S(1)}, u32[]{:S(2)}, u32[]{:S(2)}) collective-permute-start(bf16[1,128,256]{2,1,0:T(8,128)(2,1)S(1)} %get-tuple-element.84), channel_id=1, source_target_pairs={{0,8},{4,12},{8,16},{12,20},{16,24},{20,28},{1,9},{5,13},{9,17},{1... | collective-permute-start | bytes 196616 | tf_op jit(solution)/shard_map/ppermute | solution.py:14
  63.3 7.2 %collective-permute-start.7 = (bf16[1,128,256]{2,1,0:T(8,128)(2,1)S(1)}, bf16[1,128,256]{2,1,0:T(8,128)(2,1)S(1)}, u32[]{:S(2)}, u32[]{:S(2)}) collective-permute-start(bf16[1,128,256]{2,1,0:T(8,128)(2,1)S(1)} %get-tuple-element.85), channel_id=1, source_target_pairs={{0,4},{4,8},{8,12},{12,16},{16,20},{20,24},{24,28},{1,5},{5,9},{9,... | collective-permute-start | bytes 196616 | tf_op jit(solution)/shard_map/ppermute | solution.py:14
  65.2 5.3 %collective-permute-start.5 = (bf16[1,128,256]{2,1,0:T(8,128)(2,1)S(1)}, bf16[1,128,256]{2,1,0:T(8,128)(2,1)S(1)}, u32[]{:S(2)}, u32[]{:S(2)}) collective-permute-start(bf16[1,128,256]{2,1,0:T(8,128)(2,1)S(1)} %get-tuple-element.86), channel_id=1, source_target_pairs={{4,0},{8,4},{12,8},{16,12},{20,16},{24,20},{28,24},{5,1},{9,5},{13... | collective-permute-start | bytes 196616 | tf_op jit(solution)/shard_map/ppermute | solution.py:14
  67.2 7.9 %collective-permute-start.3 = (bf16[1,128,256]{2,1,0:T(8,128)(2,1)S(1)}, bf16[1,128,256]{2,1,0:T(8,128)(2,1)S(1)}, u32[]{:S(2)}, u32[]{:S(2)}) collective-permute-start(bf16[1,128,256]{2,1,0:T(8,128)(2,1)S(1)} %get-tuple-element.87), channel_id=1, source_target_pairs={{8,0},{12,4},{16,8},{20,12},{24,16},{28,20},{9,1},{13,5},{17,9},{2... | collective-permute-start | bytes 196616 | tf_op jit(solution)/shard_map/ppermute | solution.py:14
  69.2 7.8 %collective-permute-start.1 = (bf16[1,128,256]{2,1,0:T(8,128)(2,1)S(1)}, bf16[1,128,256]{2,1,0:T(8,128)(2,1)S(1)}, u32[]{:S(2)}, u32[]{:S(2)}) collective-permute-start(bf16[1,128,256]{2,1,0:T(8,128)(2,1)S(1)} %get-tuple-element.88), channel_id=1, source_target_pairs={{12,0},{16,4},{20,8},{24,12},{28,16},{13,1},{17,5},{21,9},{25,13},... | collective-permute-start | bytes 196616 | tf_op jit(solution)/shard_map/ppermute | solution.py:14
Sparse Core Ops, SparseCore 0:
  8.9 83.4 all-gather.1
  96.6 25.7 reduce-scatter.1
where the time goes:
time: 130 us; the launch traced here: 129 us
  waiting for transfers between devices  48.5 us (37%)
  between operations  36 us (28%)
  starting transfers between devices  29.8 us (23%)
  other arithmetic  6.48 us (5%)
  local copies, waits for them, and re-layouts  4.5 us (3%)
  matrix products  4.07 us (3%)
    ppermute x12, starting transfers between devices, shifted(): return lax.ppermute(x, axis, pairs)  29.7 us
    reduce_scatter x1, waiting for transfers between devices, body(): lax.psum_scatter(partial_image, 'det', scatter_dimension=1, tiled=True)  25.9 us
    all_gather x1, waiting for transfers between devices, body(): lax.all_gather(tables, 'det', axis=2, tiled=True)  15.4 us
    ppermute x12, waiting for transfers between devices, shifted(): return lax.ppermute(x, axis, pairs)  6.42 us
    another operation x14, other arithmetic  4.75 us
    dot_general x1, matrix products, body(): jnp.einsum('tfk,tkv->fv', binned, lax.all_gather(tables, 'det', axis=2, t...  4.07 us
  transfers between devices with their start and end apart: 14, of which 4 were waited for; matrix products, arithmetic and copies ran while one was open for 8% of the time, Pallas kernels for 0%

commit v1 on v0

v1 whole, which is shorter than its diff:
```python
import jax
import jax.numpy as jnp
from jax import lax
from jax.experimental import pallas as pl
from jax.experimental.pallas import tpu as pltpu
from jax.sharding import PartitionSpec as P

KWIN = 256
NTAB = 4
RANGE = 3
LANES = 128
CODE_ROWS = 8
OFFSETS = (0, 1, -1, 2, -2, 3, -3)


def rotated(x, axis, by):
    peers = lax.axis_size(axis)
    return lax.ppermute(x, axis, [(i, (i + by) % peers) for i in range(peers)])


def cut_kernel(place, starts, slots, ranges, traces, *rest):
    outs, held, sems = rest[: len(OFFSETS)], rest[-2], rest[-1]
    n_rows, width = held.shape[1], held.shape[2]
    last_base = traces.shape[2] - width
    copies, shifts = [], []
    for i, offset in enumerate(OFFSETS):
        start = starts[0, offset + RANGE]
        base = jnp.minimum(start // LANES * LANES, last_base)
        shifts.append(start - base)
        copies.append(
            pltpu.make_async_copy(
                traces.at[0, :, pl.ds(pl.multiple_of(base, LANES), width)], held.at[i], sems.at[i]
            )
        )
    for copy in copies:
        copy.start()
    for i, offset in enumerate(OFFSETS):
        target = place[0] + offset
        active = (
            (target >= 0) & (target < place[1]) & (ranges[0, 0] <= target) & (target <= ranges[0, 1])
        )
        code = jnp.where(active, slots[0, offset + RANGE], -1).astype(jnp.float32)
        outs[i][n_rows:, :] = jnp.full((CODE_ROWS, KWIN), code, jnp.float32).astype(jnp.bfloat16)
        copies[i].wait()
        back = jnp.where(shifts[i] == 0, 0, width - shifts[i])
        window = pltpu.roll(held[i], back, 1)[:, :KWIN]
        outs[i][:n_rows, :] = window.astype(jnp.bfloat16)


def bin_kernel(place, *refs):
    windows, outs = refs[: len(OFFSETS)], refs[len(OFFSETS):]
    peers = len(outs)
    rows = outs[0].shape[0]
    frames = rows * peers
    codes = [ref[frames : frames + 1, :].astype(jnp.float32) for ref in windows]
    for r in range(peers):
        first = pl.multiple_of((place[2] + r) % peers * rows, rows)
        parts = [ref[pl.ds(first, rows), :].astype(jnp.float32) for ref in windows]
        for t in range(NTAB):
            total = jnp.zeros((rows, KWIN), jnp.float32)
            for code, part in zip(codes, parts):
                total = total + jnp.where(code == t, part, 0.0)
            outs[r][:, t * KWIN : (t + 1) * KWIN] = total.astype(jnp.bfloat16)


def image_kernel(place, *refs):
    blocks, tables, out, stack = refs[:-3], refs[-3], refs[-2], refs[-1]
    peers = len(blocks)
    rows = blocks[0].shape[0]
    for r, block in enumerate(blocks):
        first = pl.multiple_of((place[2] + peers - r) % peers * rows, rows)
        stack[pl.ds(first, rows), :] = block[...]
    weights = tables[...].reshape(NTAB * KWIN, tables.shape[2])
    out[...] = jnp.dot(stack[...], weights, preferred_element_type=jnp.float32)


SMEM = pl.BlockSpec(memory_space=pltpu.SMEM)
VMEM = pl.BlockSpec(memory_space=pltpu.VMEM)
ANY = pl.BlockSpec(memory_space=pl.ANY)


def body(traces, tables, slab_range, table_slot, sample_start):
    peers = lax.axis_size("det")
    frames, voxels = traces.shape[1], tables.shape[2]
    rows = frames // peers
    place = jnp.stack(
        [lax.axis_index("slab"), jnp.int32(lax.axis_size("slab")), lax.axis_index("det")]
    ).astype(jnp.int32)
    n_off = len(OFFSETS)
    cut = pl.pallas_call(
        cut_kernel,
        in_specs=[SMEM, SMEM, SMEM, SMEM, ANY],
        out_specs=[VMEM] * n_off,
        out_shape=[jax.ShapeDtypeStruct((frames + CODE_ROWS, KWIN), jnp.bfloat16)] * n_off,
        scratch_shapes=[
            pltpu.VMEM((n_off, frames, KWIN + LANES), jnp.float32),
            pltpu.SemaphoreType.DMA((n_off,)),
        ],
        name="cut",
    )(place, sample_start, table_slot, slab_range, traces)
    arrived = [cut[0]] + [rotated(w, "slab", o) for w, o in zip(cut[1:], OFFSETS[1:])]
    pieces = pl.pallas_call(
        bin_kernel,
        in_specs=[SMEM] + [VMEM] * n_off,
        out_specs=[VMEM] * peers,
        out_shape=[jax.ShapeDtypeStruct((rows, NTAB * KWIN), jnp.bfloat16)] * peers,
        name="bin",
    )(place, *arrived)
    turns = sorted(range(1, peers), key=lambda r: (min(r, peers - r), r))
    shares = [pieces[0]] + [rotated(pieces[r], "det", r) for r in turns]
    total = shares[0].astype(jnp.float32)
    for share in shares[1:]:
        total = total + share.astype(jnp.float32)
    summed = total.astype(jnp.bfloat16)
    gathered = {r: rotated(summed, "det", r) for r in turns}
    blocks = [summed] + [gathered[r] for r in range(1, peers)]
    return pl.pallas_call(
        image_kernel,
        in_specs=[SMEM] + [VMEM] * (peers + 1),
        out_specs=VMEM,
        out_shape=jax.ShapeDtypeStruct((frames, voxels), jnp.float32),
        scratch_shapes=[pltpu.VMEM((frames, NTAB * KWIN), jnp.bfloat16)],
        name="image",
    )(place, *blocks, tables)


def solution(mesh):
    placed = (
        P(("slab", "det"), None, None),
        P("slab", None, "det"),
        P(("slab", "det"), None),
        P(("slab", "det"), None),
        P(("slab", "det"), None),
    )
    return jax.shard_map(
        body, mesh=mesh, in_specs=placed, out_specs=P(None, ("slab", "det")), check_vma=False
    )
```

time: 130 us -> 43.2 us (0.33)
  between operations: 36 us -> 0.06 us
  waiting for transfers between devices: 48.5 us -> 16.1 us
  starting transfers between devices: 29.8 us -> 15.8 us
  Pallas kernels: 0 us -> 7.61 us
  other arithmetic: 6.48 us -> 1.52 us
  matrix products: 4.07 us -> 0 us
  local copies, waits for them, and re-layouts: 4.5 us -> 1.84 us
    reduce_scatter x1 -> x0, waiting for transfers between devices: 25.9 us -> none  [body(): lax.psum_scatter(partial_image, 'det', scatter_dimension=1, tiled=True)]
    all_gather x1 -> x0, waiting for transfers between devices: 15.4 us -> none  [body(): lax.all_gather(tables, 'det', axis=2, tiled=True)]
    ppermute x12, starting transfers between devices: 29.7 us -> 15.8 us  [rotated(): return lax.ppermute(x, axis, [(i, (i + by) % peers) for i in range(peers)])]
    ppermute x12, waiting for transfers between devices: 6.42 us -> 16.1 us  [rotated(): return lax.ppermute(x, axis, [(i, (i + by) % peers) for i in range(peers)])]
    pallas_call x0 -> x3, Pallas kernels: none -> 7.61 us  [the longest x1 3.14 us: body(): pl.pallas_call(cut_kernel, in_specs=[SMEM, SMEM, SMEM, SMEM, ANY], out_sp...]
    slice x3 -> x0, local copies, waits for them, and re-layouts: 4.5 us -> none  [the longest x1 1.6 us: body(): sample_start[:, RANGE]]
    another operation x14 -> x1, other arithmetic: 4.75 us -> 0.65 us  [body(): jnp.stack([lax.axis_index('slab'), jnp.int32(lax.axis_size('slab')), lax....]
    dot_general x1 -> x0, matrix products: 4.07 us -> none  [body(): jnp.einsum('tfk,tkv->fv', binned, lax.all_gather(tables, 'det', axis=2, t...]
  transfers between devices with their start and end apart: 14 -> 12, of which waited for: 4 -> 8; matrix products, arithmetic and copies ran while one was open for 8% -> 0% of each run, Pallas kernels for 0% -> 0%
where the time goes in v1:
time: 43.2 us; the launch traced here: 42.9 us
  waiting for transfers between devices  16.1 us (37%)
  starting transfers between devices  15.8 us (37%)
  Pallas kernels  7.61 us (18%)
  local copies, waits for them, and re-layouts  1.84 us (4%)
  other arithmetic  1.52 us (4%)
    ppermute x12, waiting for transfers between devices, rotated(): return lax.ppermute(x, axis, [(i, (i + by) % peers) for i in range(peers)])  16.1 us
    ppermute x12, starting transfers between devices, rotated(): return lax.ppermute(x, axis, [(i, (i + by) % peers) for i in range(peers)])  15.8 us
    pallas_call x1, Pallas kernels, body(): pl.pallas_call(cut_kernel, in_specs=[SMEM, SMEM, SMEM, SMEM, ANY], out_sp...  3.14 us
    pallas_call x1, Pallas kernels, body(): pl.pallas_call(image_kernel, in_specs=[SMEM] + [VMEM] * (peers + 1), out_...  2.4 us
    pallas_call x1, Pallas kernels, body(): pl.pallas_call(bin_kernel, in_specs=[SMEM] + [VMEM] * n_off, out_specs=[V...  2.06 us
    unnamed x20, local copies, waits for them, and re-layouts  1.84 us
    convert_element_type x1, other arithmetic, body(): summed = total.astype(jnp.bfloat16)  0.88 us
  transfers between devices with their start and end apart: 12, of which 8 were waited for; matrix products, arithmetic and copies ran while one was open for 0% of the time, Pallas kernels for 0%

profile of v1, /device:TPU:0, one launch (start us, length us, event | category | flops | bytes accessed | tf_op | source)
XLA Modules:
  0.0 42.9 jit_solution(15515864908858320155)
XLA Ops:
  0.0 0.6 %pad_add_fusion.place = s32[3]{0:T(128)} fusion(s32[1]{0:T(128)} %bitcast.1, s32[1]{0:T(128)} %constant.9.clone.1, s32[1]{0:T(128)} %bitcast), kind=kLoop, calls=%fused_computation.1 | loop fusion | flops 6 | bytes 24 | tf_op jit(solution)/shard_map/stack | solution.py:86
  0.6 3.1 %cut.1 = (bf16[136,256]{1,0:T(8,128)(2,1)}, bf16[136,256]{1,0:T(8,128)(2,1)}, bf16[136,256]{1,0:T(8,128)(2,1)}, bf16[136,256]{1,0:T(8,128)(2,1)}, bf16[136,256]{...) custom-call(s32[3]{0:T(128)} %pad_add_fusion.place, s32[1,7]{1,0:T(1,128)} %starts.1, ...), custom_call_target="tpu_custom_call" | custom-call | tf_op jit(solution)/shard_map/cut/pallas_call | solution.py:90
  4.3 2.9 %collective-permute-start.1 = (bf16[136,256]{1,0:T(8,128)(2,1)}, bf16[136,256]{1,0:T(8,128)(2,1)S(1)}, u32[]{:S(2)}, u32[]{:S(2)}) collective-permute-start(bf16[136,256]{1,0:T(8,128)(2,1)} %get-tuple-element.18), channel_id=1, source_target_pairs={{0,28},{4,0},{8,4},{12,8},{16,12},{20,16},{24,20},{28,24},{1,29},{... | collective-permute-start | bytes 208904 | tf_op jit(solution)/shard_map/ppermute | solution.py:18
  7.3 1.3 %collective-permute-start.2 = (bf16[136,256]{1,0:T(8,128)(2,1)}, bf16[136,256]{1,0:T(8,128)(2,1)S(1)}, u32[]{:S(2)}, u32[]{:S(2)}) collective-permute-start(bf16[136,256]{1,0:T(8,128)(2,1)} %get-tuple-element.19), channel_id=1, source_target_pairs={{0,8},{4,12},{8,16},{12,20},{16,24},{20,28},{24,0},{28,4},{1,9},{5... | collective-permute-start | bytes 208904 | tf_op jit(solution)/shard_map/ppermute | solution.py:18
  8.6 1.6 %collective-permute-start.3 = (bf16[136,256]{1,0:T(8,128)(2,1)}, bf16[136,256]{1,0:T(8,128)(2,1)S(1)}, u32[]{:S(2)}, u32[]{:S(2)}) collective-permute-start(bf16[136,256]{1,0:T(8,128)(2,1)} %get-tuple-element.20), channel_id=1, source_target_pairs={{0,24},{4,28},{8,0},{12,4},{16,8},{20,12},{24,16},{28,20},{1,25},{... | collective-permute-start | bytes 208904 | tf_op jit(solution)/shard_map/ppermute | solution.py:18
  10.2 1.7 %collective-permute-start.5 = (bf16[136,256]{1,0:T(8,128)(2,1)}, bf16[136,256]{1,0:T(8,128)(2,1)S(1)}, u32[]{:S(2)}, u32[]{:S(2)}) collective-permute-start(bf16[136,256]{1,0:T(8,128)(2,1)} %get-tuple-element.22), channel_id=1, source_target_pairs={{0,20},{4,24},{8,28},{12,0},{16,4},{20,8},{24,12},{28,16},{1,21},{... | collective-permute-start | bytes 208904 | tf_op jit(solution)/shard_map/ppermute | solution.py:18
  12.0 1.7 %collective-permute-done.2.refs_3_ = bf16[136,256]{1,0:T(8,128)(2,1)S(1)} collective-permute-done((bf16[136,256]{1,0:T(8,128)(2,1)}, bf16[136,256]{1,0:T(8,128)(2,1)S(1)}, u32[]{:S(2)}, u32[]{:S(2)}) %collective-permute-start.2) | collective-permute-done | bytes 69664 | tf_op jit(solution)/shard_map/ppermute | solution.py:18
  13.7 1.3 %collective-permute-done.3.refs_4_ = bf16[136,256]{1,0:T(8,128)(2,1)S(1)} collective-permute-done((bf16[136,256]{1,0:T(8,128)(2,1)}, bf16[136,256]{1,0:T(8,128)(2,1)S(1)}, u32[]{:S(2)}, u32[]{:S(2)}) %collective-permute-start.3) | collective-permute-done | bytes 69664 | tf_op jit(solution)/shard_map/ppermute | solution.py:18
  14.9 0.6 %collective-permute-done.5.refs_6_ = bf16[136,256]{1,0:T(8,128)(2,1)S(1)} collective-permute-done((bf16[136,256]{1,0:T(8,128)(2,1)}, bf16[136,256]{1,0:T(8,128)(2,1)S(1)}, u32[]{:S(2)}, u32[]{:S(2)}) %collective-permute-start.5) | collective-permute-done | bytes 69664 | tf_op jit(solution)/shard_map/ppermute | solution.py:18
  16.1 2.1 %bin.1 = (bf16[32,1024]{1,0:T(8,128)(2,1)}, bf16[32,1024]{1,0:T(8,128)(2,1)}, bf16[32,1024]{1,0:T(8,128)(2,1)}, bf16[32,1024]{1,0:T(8,128)(2,1)}) custom-call(s32[3]{0:T(128)} %pad_add_fusion.place, bf16[136,256]{1,0:T(8,128)(2,1)} %get-tuple-element.16.refs_0_, bf16[136,256]{1,0:T(8,128)(2,1)} %copy-done.1, bf16[136,256]{1,0:T(8,128)(2,1)} %copy-done.2, ...), custom_call_target="tpu_custom_call" | custom-call | tf_op jit(solution)/shard_map/bin/pallas_call | solution.py:102
  18.2 1.7 %collective-permute-start.6 = (bf16[32,1024]{1,0:T(8,128)(2,1)}, bf16[32,1024]{1,0:T(8,128)(2,1)S(1)}, u32[]{:S(2)}, u32[]{:S(2)}) collective-permute-start(bf16[32,1024]{1,0:T(8,128)(2,1)} %get-tuple-element.24), channel_id=1, source_target_pairs={{0,1},{1,2},{2,3},{3,0},{4,5},{5,6},{6,7},{7,4},{8,9},{9,10},{10,1... | collective-permute-start | bytes 196616 | tf_op jit(solution)/shard_map/ppermute | solution.py:18
  19.9 2.1 %collective-permute-start.7 = (bf16[32,1024]{1,0:T(8,128)(2,1)}, bf16[32,1024]{1,0:T(8,128)(2,1)S(1)}, u32[]{:S(2)}, u32[]{:S(2)}) collective-permute-start(bf16[32,1024]{1,0:T(8,128)(2,1)} %get-tuple-element.25), channel_id=1, source_target_pairs={{0,3},{1,0},{2,1},{3,2},{4,7},{5,4},{6,5},{7,6},{8,11},{9,8},{10,9... | collective-permute-start | bytes 196616 | tf_op jit(solution)/shard_map/ppermute | solution.py:18
  22.0 0.9 %collective-permute-start.8 = (bf16[32,1024]{1,0:T(8,128)(2,1)}, bf16[32,1024]{1,0:T(8,128)(2,1)S(1)}, u32[]{:S(2)}, u32[]{:S(2)}) collective-permute-start(bf16[32,1024]{1,0:T(8,128)(2,1)} %get-tuple-element.26), channel_id=1, source_target_pairs={{0,2},{1,3},{2,0},{3,1},{4,6},{5,7},{6,4},{7,5},{8,10},{9,11},{10,... | collective-permute-start | bytes 196616 | tf_op jit(solution)/shard_map/ppermute | solution.py:18
  22.9 2.3 %collective-permute-done.6 = bf16[32,1024]{1,0:T(8,128)(2,1)S(1)} collective-permute-done((bf16[32,1024]{1,0:T(8,128)(2,1)}, bf16[32,1024]{1,0:T(8,128)(2,1)S(1)}, u32[]{:S(2)}, u32[]{:S(2)}) %collective-permute-start.6) | collective-permute-done | bytes 65568 | tf_op jit(solution)/shard_map/ppermute | solution.py:18
  25.2 0.9 %collective-permute-done.7 = bf16[32,1024]{1,0:T(8,128)(2,1)S(1)} collective-permute-done((bf16[32,1024]{1,0:T(8,128)(2,1)}, bf16[32,1024]{1,0:T(8,128)(2,1)S(1)}, u32[]{:S(2)}, u32[]{:S(2)}) %collective-permute-start.7) | collective-permute-done | bytes 65568 | tf_op jit(solution)/shard_map/ppermute | solution.py:18
  26.1 3.3 %collective-permute-done.8 = bf16[32,1024]{1,0:T(8,128)(2,1)S(1)} collective-permute-done((bf16[32,1024]{1,0:T(8,128)(2,1)}, bf16[32,1024]{1,0:T(8,128)(2,1)S(1)}, u32[]{:S(2)}, u32[]{:S(2)}) %collective-permute-start.8) | collective-permute-done | bytes 65568 | tf_op jit(solution)/shard_map/ppermute | solution.py:18
  29.4 0.9 %add_convert_fusion.refs_0_ = bf16[32,1024]{1,0:T(8,128)(2,1)S(1)} fusion(bf16[32,1024]{1,0:T(8,128)(2,1)S(1)} %collective-permute-done.8, bf16[32,1024]{1,0:T(8,128)(2,1)S(1)} %collective-permute-done.7, bf16[32,1024]{1,0:T(8,128)(2,1)S(1)} %collective-permute-done.6, bf16[32,1024]{1,0:T(8,128)(2,1)} %get-tuple-element.23), kind=kLoop, calls=%fused_computation | loop fusion | flops 262144 | bytes 327680 | tf_op jit(solution)/shard_map/convert_element_type | solution.py:114
  30.3 2.3 %collective-permute-start.11 = (bf16[32,1024]{1,0:T(8,128)(2,1)S(1)}, bf16[32,1024]{1,0:T(8,128)(2,1)S(1)}, u32[]{:S(2)}, u32[]{:S(2)}) collective-permute-start(bf16[32,1024]{1,0:T(8,128)(2,1)S(1)} %add_convert_fusion.refs_0_), channel_id=1, source_target_pairs={{0,3},{1,0},{2,1},{3,2},{4,7},{5,4},{6,5},{7,6},{8,11},{9,8},{10,9... | collective-permute-start | bytes 196616 | tf_op jit(solution)/shard_map/ppermute | solution.py:18
  32.5 0.6 %collective-permute-start.9 = (bf16[32,1024]{1,0:T(8,128)(2,1)S(1)}, bf16[32,1024]{1,0:T(8,128)(2,1)S(1)}, u32[]{:S(2)}, u32[]{:S(2)}) collective-permute-start(bf16[32,1024]{1,0:T(8,128)(2,1)S(1)} %add_convert_fusion.refs_0_), channel_id=1, source_target_pairs={{0,1},{1,2},{2,3},{3,0},{4,5},{5,6},{6,7},{7,4},{8,9},{9,10},{10,1... | collective-permute-start | bytes 196616 | tf_op jit(solution)/shard_map/ppermute | solution.py:18
  33.2 1.9 %collective-permute-done.11.refs_3_ = bf16[32,1024]{1,0:T(8,128)(2,1)S(1)} collective-permute-done((bf16[32,1024]{1,0:T(8,128)(2,1)S(1)}, bf16[32,1024]{1,0:T(8,128)(2,1)S(1)}, u32[]{:S(2)}, u32[]{:S(2)}) %collective-permute-start.11) | collective-permute-done | bytes 65568 | tf_op jit(solution)/shard_map/ppermute | solution.py:18
  35.0 4.3 %collective-permute-done.10.refs_2_ = bf16[32,1024]{1,0:T(8,128)(2,1)S(1)} collective-permute-done((bf16[32,1024]{1,0:T(8,128)(2,1)S(1)}, bf16[32,1024]{1,0:T(8,128)(2,1)S(1)}, u32[]{:S(2)}, u32[]{:S(2)}) %collective-permute-start.10) | collective-permute-done | bytes 65568 | tf_op jit(solution)/shard_map/ppermute | solution.py:18
  39.3 0.6 %copy-done.8 = bf16[32,1024]{1,0:T(8,128)(2,1)} copy-done((bf16[32,1024]{1,0:T(8,128)(2,1)}, bf16[32,1024]{1,0:T(8,128)(2,1)S(1)}, u32[]{:S(2)}) %copy-start.8) | copy-done | bytes 65560
  39.9 0.6 %copy-done.9 = bf16[32,1024]{1,0:T(8,128)(2,1)} copy-done((bf16[32,1024]{1,0:T(8,128)(2,1)}, bf16[32,1024]{1,0:T(8,128)(2,1)S(1)}, u32[]{:S(2)}) %copy-start.9) | copy-done | bytes 65560
  40.5 2.4 %image.1 = f32[128,512]{1,0:T(8,128)} custom-call(s32[3]{0:T(128)} %pad_add_fusion.place, bf16[32,1024]{1,0:T(8,128)(2,1)} %copy-done, bf16[32,1024]{1,0:T(8,128)(2,1)} %copy-done.9, bf16[32,1024]{1,0:T(8,128)(2,1)} %copy-done.8, bf16[32,1024]{1,0:T(8,128)(2,1)} %copy-done.7, bf16[4,256,512]{2,1,0:T(8,128)(2,1)} %refs_4_.1), custom_call_target="tpu_custom_call" | custom-call | tf_op jit(solution)/shard_map/image/pallas_call | solution.py:117
  (25 shorter events, 1.2 us)
Async XLA Ops:
  3.8 6.4 %collective-permute-start = (bf16[136,256]{1,0:T(8,128)(2,1)}, bf16[136,256]{1,0:T(8,128)(2,1)S(1)}, u32[]{:S(2)}, u32[]{:S(2)}) collective-permute-start(bf16[136,256]{1,0:T(8,128)(2,1)} %get-tuple-element.17), channel_id=1, source_target_pairs={{0,4},{4,8},{8,12},{12,16},{16,20},{20,24},{24,28},{28,0},{1,5},{5... | collective-permute-start | bytes 208904 | tf_op jit(solution)/shard_map/ppermute | solution.py:18
  4.3 7.6 %collective-permute-start.1 = (bf16[136,256]{1,0:T(8,128)(2,1)}, bf16[136,256]{1,0:T(8,128)(2,1)S(1)}, u32[]{:S(2)}, u32[]{:S(2)}) collective-permute-start(bf16[136,256]{1,0:T(8,128)(2,1)} %get-tuple-element.18), channel_id=1, source_target_pairs={{0,28},{4,0},{8,4},{12,8},{16,12},{20,16},{24,20},{28,24},{1,29},{... | collective-permute-start | bytes 208904 | tf_op jit(solution)/shard_map/ppermute | solution.py:18
  7.3 6.4 %collective-permute-start.2 = (bf16[136,256]{1,0:T(8,128)(2,1)}, bf16[136,256]{1,0:T(8,128)(2,1)S(1)}, u32[]{:S(2)}, u32[]{:S(2)}) collective-permute-start(bf16[136,256]{1,0:T(8,128)(2,1)} %get-tuple-element.19), channel_id=1, source_target_pairs={{0,8},{4,12},{8,16},{12,20},{16,24},{20,28},{24,0},{28,4},{1,9},{5... | collective-permute-start | bytes 208904 | tf_op jit(solution)/shard_map/ppermute | solution.py:18
  8.6 6.4 %collective-permute-start.3 = (bf16[136,256]{1,0:T(8,128)(2,1)}, bf16[136,256]{1,0:T(8,128)(2,1)S(1)}, u32[]{:S(2)}, u32[]{:S(2)}) collective-permute-start(bf16[136,256]{1,0:T(8,128)(2,1)} %get-tuple-element.20), channel_id=1, source_target_pairs={{0,24},{4,28},{8,0},{12,4},{16,8},{20,12},{24,16},{28,20},{1,25},{... | collective-permute-start | bytes 208904 | tf_op jit(solution)/shard_map/ppermute | solution.py:18
  10.2 4.7 %collective-permute-start.4 = (bf16[136,256]{1,0:T(8,128)(2,1)}, bf16[136,256]{1,0:T(8,128)(2,1)S(1)}, u32[]{:S(2)}, u32[]{:S(2)}) collective-permute-start(bf16[136,256]{1,0:T(8,128)(2,1)} %get-tuple-element.21), channel_id=1, source_target_pairs={{0,12},{4,16},{8,20},{12,24},{16,28},{20,0},{24,4},{28,8},{1,13},{... | collective-permute-start | bytes 208904 | tf_op jit(solution)/shard_map/ppermute | solution.py:18
  10.2 5.3 %copy-start.1 = (bf16[136,256]{1,0:T(8,128)(2,1)}, bf16[136,256]{1,0:T(8,128)(2,1)S(1)}, u32[]{:S(2)}) copy-start(bf16[136,256]{1,0:T(8,128)(2,1)S(1)} %collective-permute-done.refs_1_) | copy-start | bytes 208900
  10.2 5.3 %collective-permute-start.5 = (bf16[136,256]{1,0:T(8,128)(2,1)}, bf16[136,256]{1,0:T(8,128)(2,1)S(1)}, u32[]{:S(2)}, u32[]{:S(2)}) collective-permute-start(bf16[136,256]{1,0:T(8,128)(2,1)} %get-tuple-element.22), channel_id=1, source_target_pairs={{0,20},{4,24},{8,28},{12,0},{16,4},{20,8},{24,12},{28,16},{1,21},{... | collective-permute-start | bytes 208904 | tf_op jit(solution)/shard_map/ppermute | solution.py:18
  12.0 3.6 %copy-start.2 = (bf16[136,256]{1,0:T(8,128)(2,1)}, bf16[136,256]{1,0:T(8,128)(2,1)S(1)}, u32[]{:S(2)}) copy-start(bf16[136,256]{1,0:T(8,128)(2,1)S(1)} %collective-permute-done.1.refs_2_) | copy-start | bytes 208900
  13.6 1.9 %copy-start.3 = (bf16[136,256]{1,0:T(8,128)(2,1)}, bf16[136,256]{1,0:T(8,128)(2,1)S(1)}, u32[]{:S(2)}) copy-start(bf16[136,256]{1,0:T(8,128)(2,1)S(1)} %collective-permute-done.2.refs_3_) | copy-start | bytes 208900
  14.9 0.6 %copy-start.4 = (bf16[136,256]{1,0:T(8,128)(2,1)}, bf16[136,256]{1,0:T(8,128)(2,1)S(1)}, u32[]{:S(2)}) copy-start(bf16[136,256]{1,0:T(8,128)(2,1)S(1)} %collective-permute-done.3.refs_4_) | copy-start | bytes 208900
  14.9 0.7 %copy-start.5 = (bf16[136,256]{1,0:T(8,128)(2,1)}, bf16[136,256]{1,0:T(8,128)(2,1)S(1)}, u32[]{:S(2)}) copy-start(bf16[136,256]{1,0:T(8,128)(2,1)S(1)} %collective-permute-done.4.refs_5_) | copy-start | bytes 208900
  15.5 0.6 %copy-start.6 = (bf16[136,256]{1,0:T(8,128)(2,1)}, bf16[136,256]{1,0:T(8,128)(2,1)S(1)}, u32[]{:S(2)}) copy-start(bf16[136,256]{1,0:T(8,128)(2,1)S(1)} %collective-permute-done.5.refs_6_) | copy-start | bytes 208900
  18.2 7.0 %collective-permute-start.6 = (bf16[32,1024]{1,0:T(8,128)(2,1)}, bf16[32,1024]{1,0:T(8,128)(2,1)S(1)}, u32[]{:S(2)}, u32[]{:S(2)}) collective-permute-start(bf16[32,1024]{1,0:T(8,128)(2,1)} %get-tuple-element.24), channel_id=1, source_target_pairs={{0,1},{1,2},{2,3},{3,0},{4,5},{5,6},{6,7},{7,4},{8,9},{9,10},{10,1... | collective-permute-start | bytes 196616 | tf_op jit(solution)/shard_map/ppermute | solution.py:18
  19.9 6.2 %collective-permute-start.7 = (bf16[32,1024]{1,0:T(8,128)(2,1)}, bf16[32,1024]{1,0:T(8,128)(2,1)S(1)}, u32[]{:S(2)}, u32[]{:S(2)}) collective-permute-start(bf16[32,1024]{1,0:T(8,128)(2,1)} %get-tuple-element.25), channel_id=1, source_target_pairs={{0,3},{1,0},{2,1},{3,2},{4,7},{5,4},{6,5},{7,6},{8,11},{9,8},{10,9... | collective-permute-start | bytes 196616 | tf_op jit(solution)/shard_map/ppermute | solution.py:18
  22.0 7.4 %collective-permute-start.8 = (bf16[32,1024]{1,0:T(8,128)(2,1)}, bf16[32,1024]{1,0:T(8,128)(2,1)S(1)}, u32[]{:S(2)}, u32[]{:S(2)}) collective-permute-start(bf16[32,1024]{1,0:T(8,128)(2,1)} %get-tuple-element.26), channel_id=1, source_target_pairs={{0,2},{1,3},{2,0},{3,1},{4,6},{5,7},{6,4},{7,5},{8,10},{9,11},{10,... | collective-permute-start | bytes 196616 | tf_op jit(solution)/shard_map/ppermute | solution.py:18
  30.3 9.1 %copy-start = (bf16[32,1024]{1,0:T(8,128)(2,1)}, bf16[32,1024]{1,0:T(8,128)(2,1)S(1)}, u32[]{:S(2)}) copy-start(bf16[32,1024]{1,0:T(8,128)(2,1)S(1)} %add_convert_fusion.refs_0_) | copy-start | bytes 196612
  30.3 4.8 %collective-permute-start.11 = (bf16[32,1024]{1,0:T(8,128)(2,1)S(1)}, bf16[32,1024]{1,0:T(8,128)(2,1)S(1)}, u32[]{:S(2)}, u32[]{:S(2)}) collective-permute-start(bf16[32,1024]{1,0:T(8,128)(2,1)S(1)} %add_convert_fusion.refs_0_), channel_id=1, source_target_pairs={{0,3},{1,0},{2,1},{3,2},{4,7},{5,4},{6,5},{7,6},{8,11},{9,8},{10,9... | collective-permute-start | bytes 196616 | tf_op jit(solution)/shard_map/ppermute | solution.py:18
  32.5 6.8 %collective-permute-start.10 = (bf16[32,1024]{1,0:T(8,128)(2,1)S(1)}, bf16[32,1024]{1,0:T(8,128)(2,1)S(1)}, u32[]{:S(2)}, u32[]{:S(2)}) collective-permute-start(bf16[32,1024]{1,0:T(8,128)(2,1)S(1)} %add_convert_fusion.refs_0_), channel_id=1, source_target_pairs={{0,2},{1,3},{2,0},{3,1},{4,6},{5,7},{6,4},{7,5},{8,10},{9,11},{10,... | collective-permute-start | bytes 196616 | tf_op jit(solution)/shard_map/ppermute | solution.py:18
  32.5 6.8 %collective-permute-start.9 = (bf16[32,1024]{1,0:T(8,128)(2,1)S(1)}, bf16[32,1024]{1,0:T(8,128)(2,1)S(1)}, u32[]{:S(2)}, u32[]{:S(2)}) collective-permute-start(bf16[32,1024]{1,0:T(8,128)(2,1)S(1)} %add_convert_fusion.refs_0_), channel_id=1, source_target_pairs={{0,1},{1,2},{2,3},{3,0},{4,5},{5,6},{6,7},{7,4},{8,9},{9,10},{10,1... | collective-permute-start | bytes 196616 | tf_op jit(solution)/shard_map/ppermute | solution.py:18
  35.0 4.3 %copy-start.7 = (bf16[32,1024]{1,0:T(8,128)(2,1)}, bf16[32,1024]{1,0:T(8,128)(2,1)S(1)}, u32[]{:S(2)}) copy-start(bf16[32,1024]{1,0:T(8,128)(2,1)S(1)} %collective-permute-done.11.refs_3_) | copy-start | bytes 196612
  39.3 0.6 %copy-start.8 = (bf16[32,1024]{1,0:T(8,128)(2,1)}, bf16[32,1024]{1,0:T(8,128)(2,1)S(1)}, u32[]{:S(2)}) copy-start(bf16[32,1024]{1,0:T(8,128)(2,1)S(1)} %collective-permute-done.10.refs_2_) | copy-start | bytes 196612
  39.9 0.6 %copy-start.9 = (bf16[32,1024]{1,0:T(8,128)(2,1)}, bf16[32,1024]{1,0:T(8,128)(2,1)S(1)}, u32[]{:S(2)}) copy-start(bf16[32,1024]{1,0:T(8,128)(2,1)S(1)} %collective-permute-done.9.refs_1_) | copy-start | bytes 196612

commit v2 on v1

--- a/solution.py
+++ b/solution.py
@@ -18,7 +18,11 @@
     return lax.ppermute(x, axis, [(i, (i + by) % peers) for i in range(peers)])
 
 
-def cut_kernel(place, starts, slots, ranges, traces, *rest):
+def near(x):
+    return pltpu.with_memory_space_constraint(x, pltpu.VMEM)
+
+
+def cut_kernel(starts, slots, ranges, traces, *rest):
     outs, held, sems = rest[: len(OFFSETS)], rest[-2], rest[-1]
     n_rows, width = held.shape[1], held.shape[2]
     last_base = traces.shape[2] - width
@@ -35,9 +39,9 @@
     for copy in copies:
         copy.start()
     for i, offset in enumerate(OFFSETS):
-        target = place[0] + offset
+        target = lax.axis_index("slab") + offset
         active = (
-            (target >= 0) & (target < place[1]) & (ranges[0, 0] <= target) & (target <= ranges[0, 1])
+            (target >= 0) & (target < lax.axis_size("slab")) & (ranges[0, 0] <= target) & (target <= ranges[0, 1])
         )
         code = jnp.where(active, slots[0, offset + RANGE], -1).astype(jnp.float32)
         outs[i][n_rows:, :] = jnp.full((CODE_ROWS, KWIN), code, jnp.float32).astype(jnp.bfloat16)
@@ -47,14 +51,14 @@
         outs[i][:n_rows, :] = window.astype(jnp.bfloat16)
 
 
-def bin_kernel(place, *refs):
+def bin_kernel(*refs):
     windows, outs = refs[: len(OFFSETS)], refs[len(OFFSETS):]
     peers = len(outs)
     rows = outs[0].shape[0]
     frames = rows * peers
     codes = [ref[frames : frames + 1, :].astype(jnp.float32) for ref in windows]
     for r in range(peers):
-        first = pl.multiple_of((place[2] + r) % peers * rows, rows)
+        first = pl.multiple_of((lax.axis_index("det") + r) % peers * rows, rows)
         parts = [ref[pl.ds(first, rows), :].astype(jnp.float32) for ref in windows]
         for t in range(NTAB):
             total = jnp.zeros((rows, KWIN), jnp.float32)
@@ -63,12 +67,12 @@
             outs[r][:, t * KWIN : (t + 1) * KWIN] = total.astype(jnp.bfloat16)
 
 
-def image_kernel(place, *refs):
+def image_kernel(*refs):
     blocks, tables, out, stack = refs[:-3], refs[-3], refs[-2], refs[-1]
     peers = len(blocks)
     rows = blocks[0].shape[0]
     for r, block in enumerate(blocks):
-        first = pl.multiple_of((place[2] + peers - r) % peers * rows, rows)
+        first = pl.multiple_of((lax.axis_index("det") + peers - r) % peers * rows, rows)
         stack[pl.ds(first, rows), :] = block[...]
     weights = tables[...].reshape(NTAB * KWIN, tables.shape[2])
     out[...] = jnp.dot(stack[...], weights, preferred_element_type=jnp.float32)
@@ -83,29 +87,26 @@
     peers = lax.axis_size("det")
     frames, voxels = traces.shape[1], tables.shape[2]
     rows = frames // peers
-    place = jnp.stack(
-        [lax.axis_index("slab"), jnp.int32(lax.axis_size("slab")), lax.axis_index("det")]
-    ).astype(jnp.int32)
     n_off = len(OFFSETS)
     cut = pl.pallas_call(
         cut_kernel,
-        in_specs=[SMEM, SMEM, SMEM, SMEM, ANY],
+        in_specs=[SMEM, SMEM, SMEM, ANY],
         out_specs=[VMEM] * n_off,
-        out_shape=[jax.ShapeDtypeStruct((frames + CODE_ROWS, KWIN), jnp.bfloat16)] * n_off,
+        out_shape=[pltpu.VMEM((frames + CODE_ROWS, KWIN), jnp.bfloat16)] * n_off,
         scratch_shapes=[
             pltpu.VMEM((n_off, frames, KWIN + LANES), jnp.float32),
             pltpu.SemaphoreType.DMA((n_off,)),
         ],
         name="cut",
-    )(place, sample_start, table_slot, slab_range, traces)
+    )(sample_start, table_slot, slab_range, traces)
     arrived = [cut[0]] + [rotated(w, "slab", o) for w, o in zip(cut[1:], OFFSETS[1:])]
     pieces = pl.pallas_call(
         bin_kernel,
-        in_specs=[SMEM] + [VMEM] * n_off,
+        in_specs=[VMEM] * n_off,
         out_specs=[VMEM] * peers,
-        out_shape=[jax.ShapeDtypeStruct((rows, NTAB * KWIN), jnp.bfloat16)] * peers,
+        out_shape=[pltpu.VMEM((rows, NTAB * KWIN), jnp.bfloat16)] * peers,
         name="bin",
-    )(place, *arrived)
+    )(*map(near, arrived))
     turns = sorted(range(1, peers), key=lambda r: (min(r, peers - r), r))
     shares = [pieces[0]] + [rotated(pieces[r], "det", r) for r in turns]
     total = shares[0].astype(jnp.float32)
@@ -116,12 +117,12 @@
     blocks = [summed] + [gathered[r] for r in range(1, peers)]
     return pl.pallas_call(
         image_kernel,
-        in_specs=[SMEM] + [VMEM] * (peers + 1),
+        in_specs=[VMEM] * (peers + 1),
         out_specs=VMEM,
         out_shape=jax.ShapeDtypeStruct((frames, voxels), jnp.float32),
         scratch_shapes=[pltpu.VMEM((frames, NTAB * KWIN), jnp.bfloat16)],
         name="image",
-    )(place, *blocks, tables)
+    )(*map(near, blocks), near(tables))
 
 
 def solution(mesh):

time: 43.2 us -> 35.8 us (0.83)
  Pallas kernels: 7.61 us -> 4 us
  local copies, waits for them, and re-layouts: 1.84 us -> 0.01 us
  other arithmetic: 1.52 us -> 0.04 us
  waiting for transfers between devices: 16.1 us -> 15.6 us
    pallas_call x3, Pallas kernels: 7.61 us -> 4 us  [the longest x1 2.63 us: body(): pl.pallas_call(cut_kernel, in_specs=[SMEM, SMEM, SMEM, ANY], out_specs=[V...]
    unnamed x20 -> x2, local copies, waits for them, and re-layouts: 1.84 us -> 0.01 us
    convert_element_type x1, other arithmetic: 0.88 us -> 0.04 us  [body(): summed = total.astype(jnp.bfloat16)]
    another operation x1 -> x0, other arithmetic: 0.65 us -> none  [body(): jnp.stack([lax.axis_index('slab'), jnp.int32(lax.axis_size('slab')), lax....]
    ppermute x12, waiting for transfers between devices: 16.1 us -> 15.6 us  [rotated(): return lax.ppermute(x, axis, [(i, (i + by) % peers) for i in range(peers)])]
where the time goes in v2:
time: 35.8 us; the launch traced here: 35.7 us
  starting transfers between devices  16.1 us (45%)
  waiting for transfers between devices  15.6 us (44%)
  Pallas kernels  4 us (11%)
    ppermute x12, starting transfers between devices, rotated(): return lax.ppermute(x, axis, [(i, (i + by) % peers) for i in range(peers)])  16.1 us
    ppermute x12, waiting for transfers between devices, rotated(): return lax.ppermute(x, axis, [(i, (i + by) % peers) for i in range(peers)])  15.6 us
    pallas_call x1, Pallas kernels, body(): pl.pallas_call(cut_kernel, in_specs=[SMEM, SMEM, SMEM, ANY], out_specs=[V...  2.63 us
    pallas_call x1, Pallas kernels, body(): pl.pallas_call(image_kernel, in_specs=[VMEM] * (peers + 1), out_specs=VME...  1.03 us
  transfers between devices with their start and end apart: 12, of which 8 were waited for; matrix products, arithmetic and copies ran while one was open for 0% of the time, Pallas kernels for 0%

profile of v2, /device:TPU:0, one launch (start us, length us, event | category | flops | bytes accessed | tf_op | source)
XLA Modules:
  0.0 35.7 jit_solution(18032114040497935668)
XLA Ops:
  0.0 2.6 %cut.1 = (bf16[136,256]{1,0:T(8,128)(2,1)S(1)}, bf16[136,256]{1,0:T(8,128)(2,1)S(1)}, bf16[136,256]{1,0:T(8,128)(2,1)S(1)}, bf16[136,256]{1,0:T(8,128)(2,1)S(1)}...) custom-call(s32[1,7]{1,0:T(1,128)} %starts.1, s32[1,7]{1,0:T(1,128)} %slots.1, ...), custom_call_target="tpu_custom_call" | custom-call | tf_op jit(solution)/shard_map/cut/pallas_call | solution.py:91
  2.6 0.5 %collective-permute-start = (bf16[136,256]{1,0:T(8,128)(2,1)S(1)}, bf16[136,256]{1,0:T(8,128)(2,1)S(1)}, u32[]{:S(2)}, u32[]{:S(2)}) collective-permute-start(bf16[136,256]{1,0:T(8,128)(2,1)S(1)} %get-tuple-element.17), channel_id=1, source_target_pairs={{0,4},{4,8},{8,12},{12,16},{16,20},{20,24},{24,28},{28,0},{1,5},{5... | collective-permute-start | bytes 208904 | tf_op jit(solution)/shard_map/ppermute | solution.py:18
  3.2 2.9 %collective-permute-start.1 = (bf16[136,256]{1,0:T(8,128)(2,1)S(1)}, bf16[136,256]{1,0:T(8,128)(2,1)S(1)}, u32[]{:S(2)}, u32[]{:S(2)}) collective-permute-start(bf16[136,256]{1,0:T(8,128)(2,1)S(1)} %get-tuple-element.18), channel_id=1, source_target_pairs={{0,28},{4,0},{8,4},{12,8},{16,12},{20,16},{24,20},{28,24},{1,29},{... | collective-permute-start | bytes 208904 | tf_op jit(solution)/shard_map/ppermute | solution.py:18
  6.1 1.3 %collective-permute-start.2 = (bf16[136,256]{1,0:T(8,128)(2,1)S(1)}, bf16[136,256]{1,0:T(8,128)(2,1)S(1)}, u32[]{:S(2)}, u32[]{:S(2)}) collective-permute-start(bf16[136,256]{1,0:T(8,128)(2,1)S(1)} %get-tuple-element.19), channel_id=1, source_target_pairs={{0,8},{4,12},{8,16},{12,20},{16,24},{20,28},{24,0},{28,4},{1,9},{5... | collective-permute-start | bytes 208904 | tf_op jit(solution)/shard_map/ppermute | solution.py:18
  7.4 1.6 %collective-permute-start.3 = (bf16[136,256]{1,0:T(8,128)(2,1)S(1)}, bf16[136,256]{1,0:T(8,128)(2,1)S(1)}, u32[]{:S(2)}, u32[]{:S(2)}) collective-permute-start(bf16[136,256]{1,0:T(8,128)(2,1)S(1)} %get-tuple-element.20), channel_id=1, source_target_pairs={{0,24},{4,28},{8,0},{12,4},{16,8},{20,12},{24,16},{28,20},{1,25},{... | collective-permute-start | bytes 208904 | tf_op jit(solution)/shard_map/ppermute | solution.py:18
  9.0 0.0 collective-permute-start.4
  9.0 0.0 collective-permute-done.refs_1_
  9.1 1.7 %collective-permute-start.5 = (bf16[136,256]{1,0:T(8,128)(2,1)S(1)}, bf16[136,256]{1,0:T(8,128)(2,1)S(1)}, u32[]{:S(2)}, u32[]{:S(2)}) collective-permute-start(bf16[136,256]{1,0:T(8,128)(2,1)S(1)} %get-tuple-element.22), channel_id=1, source_target_pairs={{0,20},{4,24},{8,28},{12,0},{16,4},{20,8},{24,12},{28,16},{1,21},{... | collective-permute-start | bytes 208904 | tf_op jit(solution)/shard_map/ppermute | solution.py:18
  10.8 1.5 %collective-permute-done.2.refs_3_ = bf16[136,256]{1,0:T(8,128)(2,1)S(1)} collective-permute-done((bf16[136,256]{1,0:T(8,128)(2,1)S(1)}, bf16[136,256]{1,0:T(8,128)(2,1)S(1)}, u32[]{:S(2)}, u32[]{:S(2)}) %collective-permute-start.2) | collective-permute-done | bytes 69664 | tf_op jit(solution)/shard_map/ppermute | solution.py:18
  12.3 1.3 %collective-permute-done.3.refs_4_ = bf16[136,256]{1,0:T(8,128)(2,1)S(1)} collective-permute-done((bf16[136,256]{1,0:T(8,128)(2,1)S(1)}, bf16[136,256]{1,0:T(8,128)(2,1)S(1)}, u32[]{:S(2)}, u32[]{:S(2)}) %collective-permute-start.3) | collective-permute-done | bytes 69664 | tf_op jit(solution)/shard_map/ppermute | solution.py:18
  13.6 0.5 %collective-permute-done.5.refs_6_ = bf16[136,256]{1,0:T(8,128)(2,1)S(1)} collective-permute-done((bf16[136,256]{1,0:T(8,128)(2,1)S(1)}, bf16[136,256]{1,0:T(8,128)(2,1)S(1)}, u32[]{:S(2)}, u32[]{:S(2)}) %collective-permute-start.5) | collective-permute-done | bytes 69664 | tf_op jit(solution)/shard_map/ppermute | solution.py:18
  14.0 0.3 bin.1
  14.4 1.8 %collective-permute-start.6 = (bf16[32,1024]{1,0:T(8,128)(2,1)S(1)}, bf16[32,1024]{1,0:T(8,128)(2,1)S(1)}, u32[]{:S(2)}, u32[]{:S(2)}) collective-permute-start(bf16[32,1024]{1,0:T(8,128)(2,1)S(1)} %get-tuple-element.24), channel_id=1, source_target_pairs={{0,1},{1,2},{2,3},{3,0},{4,5},{5,6},{6,7},{7,4},{8,9},{9,10},{10,1... | collective-permute-start | bytes 196616 | tf_op jit(solution)/shard_map/ppermute | solution.py:18
  16.2 2.1 %collective-permute-start.7 = (bf16[32,1024]{1,0:T(8,128)(2,1)S(1)}, bf16[32,1024]{1,0:T(8,128)(2,1)S(1)}, u32[]{:S(2)}, u32[]{:S(2)}) collective-permute-start(bf16[32,1024]{1,0:T(8,128)(2,1)S(1)} %get-tuple-element.25), channel_id=1, source_target_pairs={{0,3},{1,0},{2,1},{3,2},{4,7},{5,4},{6,5},{7,6},{8,11},{9,8},{10,9... | collective-permute-start | bytes 196616 | tf_op jit(solution)/shard_map/ppermute | solution.py:18
  18.3 0.9 %collective-permute-start.8 = (bf16[32,1024]{1,0:T(8,128)(2,1)S(1)}, bf16[32,1024]{1,0:T(8,128)(2,1)S(1)}, u32[]{:S(2)}, u32[]{:S(2)}) collective-permute-start(bf16[32,1024]{1,0:T(8,128)(2,1)S(1)} %get-tuple-element.26), channel_id=1, source_target_pairs={{0,2},{1,3},{2,0},{3,1},{4,6},{5,7},{6,4},{7,5},{8,10},{9,11},{10,... | collective-permute-start | bytes 196616 | tf_op jit(solution)/shard_map/ppermute | solution.py:18
  19.2 1.9 %collective-permute-done.6 = bf16[32,1024]{1,0:T(8,128)(2,1)S(1)} collective-permute-done((bf16[32,1024]{1,0:T(8,128)(2,1)S(1)}, bf16[32,1024]{1,0:T(8,128)(2,1)S(1)}, u32[]{:S(2)}, u32[]{:S(2)}) %collective-permute-start.6) | collective-permute-done | bytes 65568 | tf_op jit(solution)/shard_map/ppermute | solution.py:18
  21.1 1.1 %collective-permute-done.7 = bf16[32,1024]{1,0:T(8,128)(2,1)S(1)} collective-permute-done((bf16[32,1024]{1,0:T(8,128)(2,1)S(1)}, bf16[32,1024]{1,0:T(8,128)(2,1)S(1)}, u32[]{:S(2)}, u32[]{:S(2)}) %collective-permute-start.7) | collective-permute-done | bytes 65568 | tf_op jit(solution)/shard_map/ppermute | solution.py:18
  22.2 3.2 %collective-permute-done.8 = bf16[32,1024]{1,0:T(8,128)(2,1)S(1)} collective-permute-done((bf16[32,1024]{1,0:T(8,128)(2,1)S(1)}, bf16[32,1024]{1,0:T(8,128)(2,1)S(1)}, u32[]{:S(2)}, u32[]{:S(2)}) %collective-permute-start.8) | collective-permute-done | bytes 65568 | tf_op jit(solution)/shard_map/ppermute | solution.py:18
  25.5 2.4 %collective-permute-start.11 = (bf16[32,1024]{1,0:T(8,128)(2,1)S(1)}, bf16[32,1024]{1,0:T(8,128)(2,1)S(1)}, u32[]{:S(2)}, u32[]{:S(2)}) collective-permute-start(bf16[32,1024]{1,0:T(8,128)(2,1)S(1)} %add_convert_fusion.refs_0_), channel_id=1, source_target_pairs={{0,3},{1,0},{2,1},{3,2},{4,7},{5,4},{6,5},{7,6},{8,11},{9,8},{10,9... | collective-permute-start | bytes 196616 | tf_op jit(solution)/shard_map/ppermute | solution.py:18
  27.9 0.6 %collective-permute-start.9 = (bf16[32,1024]{1,0:T(8,128)(2,1)S(1)}, bf16[32,1024]{1,0:T(8,128)(2,1)S(1)}, u32[]{:S(2)}, u32[]{:S(2)}) collective-permute-start(bf16[32,1024]{1,0:T(8,128)(2,1)S(1)} %add_convert_fusion.refs_0_), channel_id=1, source_target_pairs={{0,1},{1,2},{2,3},{3,0},{4,5},{5,6},{6,7},{7,4},{8,9},{9,10},{10,1... | collective-permute-start | bytes 196616 | tf_op jit(solution)/shard_map/ppermute | solution.py:18
  28.5 1.9 %collective-permute-done.11.refs_3_ = bf16[32,1024]{1,0:T(8,128)(2,1)S(1)} collective-permute-done((bf16[32,1024]{1,0:T(8,128)(2,1)S(1)}, bf16[32,1024]{1,0:T(8,128)(2,1)S(1)}, u32[]{:S(2)}, u32[]{:S(2)}) %collective-permute-start.11) | collective-permute-done | bytes 65568 | tf_op jit(solution)/shard_map/ppermute | solution.py:18
  30.4 4.3 %collective-permute-done.10.refs_2_ = bf16[32,1024]{1,0:T(8,128)(2,1)S(1)} collective-permute-done((bf16[32,1024]{1,0:T(8,128)(2,1)S(1)}, bf16[32,1024]{1,0:T(8,128)(2,1)S(1)}, u32[]{:S(2)}, u32[]{:S(2)}) %collective-permute-start.10) | collective-permute-done | bytes 65568 | tf_op jit(solution)/shard_map/ppermute | solution.py:18
  34.7 0.0 collective-permute-done.9.refs_1_
  34.7 1.0 %image.1 = f32[128,512]{1,0:T(8,128)} custom-call(bf16[32,1024]{1,0:T(8,128)(2,1)S(1)} %add_convert_fusion.refs_0_, bf16[32,1024]{1,0:T(8,128)(2,1)S(1)} %collective-permute-done.9.refs_1_, bf16[32,1024]{1,0:T(8,128)(2,1)S(1)} %collective-permute-done.10.refs_2_, bf16[32,1024]{1,0:T(8,128)(2,1)S(1)} %collective-permute-done.11.refs_3_, ...), custom_call_target="tpu_custom_call" | custom-call | tf_op jit(solution)/shard_map/image/pallas_call | solution.py:118
  (6 shorter events, 0.0 us)
Async XLA Ops:
  0.0 34.7 %copy-start = (bf16[4,256,512]{2,1,0:T(8,128)(2,1)S(1)}, bf16[4,256,512]{2,1,0:T(8,128)(2,1)}, u32[]{:S(2)}) copy-start(bf16[4,256,512]{2,1,0:T(8,128)(2,1)} %refs_4_.1) | copy-start | bytes 3145732
  2.6 6.4 %collective-permute-start = (bf16[136,256]{1,0:T(8,128)(2,1)S(1)}, bf16[136,256]{1,0:T(8,128)(2,1)S(1)}, u32[]{:S(2)}, u32[]{:S(2)}) collective-permute-start(bf16[136,256]{1,0:T(8,128)(2,1)S(1)} %get-tuple-element.17), channel_id=1, source_target_pairs={{0,4},{4,8},{8,12},{12,16},{16,20},{20,24},{24,28},{28,0},{1,5},{5... | collective-permute-start | bytes 208904 | tf_op jit(solution)/shard_map/ppermute | solution.py:18
  3.2 7.6 %collective-permute-start.1 = (bf16[136,256]{1,0:T(8,128)(2,1)S(1)}, bf16[136,256]{1,0:T(8,128)(2,1)S(1)}, u32[]{:S(2)}, u32[]{:S(2)}) collective-permute-start(bf16[136,256]{1,0:T(8,128)(2,1)S(1)} %get-tuple-element.18), channel_id=1, source_target_pairs={{0,28},{4,0},{8,4},{12,8},{16,12},{20,16},{24,20},{28,24},{1,29},{... | collective-permute-start | bytes 208904 | tf_op jit(solution)/shard_map/ppermute | solution.py:18
  6.1 6.2 %collective-permute-start.2 = (bf16[136,256]{1,0:T(8,128)(2,1)S(1)}, bf16[136,256]{1,0:T(8,128)(2,1)S(1)}, u32[]{:S(2)}, u32[]{:S(2)}) collective-permute-start(bf16[136,256]{1,0:T(8,128)(2,1)S(1)} %get-tuple-element.19), channel_id=1, source_target_pairs={{0,8},{4,12},{8,16},{12,20},{16,24},{20,28},{24,0},{28,4},{1,9},{5... | collective-permute-start | bytes 208904 | tf_op jit(solution)/shard_map/ppermute | solution.py:18
  7.4 6.2 %collective-permute-start.3 = (bf16[136,256]{1,0:T(8,128)(2,1)S(1)}, bf16[136,256]{1,0:T(8,128)(2,1)S(1)}, u32[]{:S(2)}, u32[]{:S(2)}) collective-permute-start(bf16[136,256]{1,0:T(8,128)(2,1)S(1)} %get-tuple-element.20), channel_id=1, source_target_pairs={{0,24},{4,28},{8,0},{12,4},{16,8},{20,12},{24,16},{28,20},{1,25},{... | collective-permute-start | bytes 208904 | tf_op jit(solution)/shard_map/ppermute | solution.py:18
  9.0 4.5 %collective-permute-start.4 = (bf16[136,256]{1,0:T(8,128)(2,1)S(1)}, bf16[136,256]{1,0:T(8,128)(2,1)S(1)}, u32[]{:S(2)}, u32[]{:S(2)}) collective-permute-start(bf16[136,256]{1,0:T(8,128)(2,1)S(1)} %get-tuple-element.21), channel_id=1, source_target_pairs={{0,12},{4,16},{8,20},{12,24},{16,28},{20,0},{24,4},{28,8},{1,13},{... | collective-permute-start | bytes 208904 | tf_op jit(solution)/shard_map/ppermute | solution.py:18
  9.1 5.0 %collective-permute-start.5 = (bf16[136,256]{1,0:T(8,128)(2,1)S(1)}, bf16[136,256]{1,0:T(8,128)(2,1)S(1)}, u32[]{:S(2)}, u32[]{:S(2)}) collective-permute-start(bf16[136,256]{1,0:T(8,128)(2,1)S(1)} %get-tuple-element.22), channel_id=1, source_target_pairs={{0,20},{4,24},{8,28},{12,0},{16,4},{20,8},{24,12},{28,16},{1,21},{... | collective-permute-start | bytes 208904 | tf_op jit(solution)/shard_map/ppermute | solution.py:18
  14.4 6.8 %collective-permute-start.6 = (bf16[32,1024]{1,0:T(8,128)(2,1)S(1)}, bf16[32,1024]{1,0:T(8,128)(2,1)S(1)}, u32[]{:S(2)}, u32[]{:S(2)}) collective-permute-start(bf16[32,1024]{1,0:T(8,128)(2,1)S(1)} %get-tuple-element.24), channel_id=1, source_target_pairs={{0,1},{1,2},{2,3},{3,0},{4,5},{5,6},{6,7},{7,4},{8,9},{9,10},{10,1... | collective-permute-start | bytes 196616 | tf_op jit(solution)/shard_map/ppermute | solution.py:18
  16.2 6.0 %collective-permute-start.7 = (bf16[32,1024]{1,0:T(8,128)(2,1)S(1)}, bf16[32,1024]{1,0:T(8,128)(2,1)S(1)}, u32[]{:S(2)}, u32[]{:S(2)}) collective-permute-start(bf16[32,1024]{1,0:T(8,128)(2,1)S(1)} %get-tuple-element.25), channel_id=1, source_target_pairs={{0,3},{1,0},{2,1},{3,2},{4,7},{5,4},{6,5},{7,6},{8,11},{9,8},{10,9... | collective-permute-start | bytes 196616 | tf_op jit(solution)/shard_map/ppermute | solution.py:18
  18.3 7.1 %collective-permute-start.8 = (bf16[32,1024]{1,0:T(8,128)(2,1)S(1)}, bf16[32,1024]{1,0:T(8,128)(2,1)S(1)}, u32[]{:S(2)}, u32[]{:S(2)}) collective-permute-start(bf16[32,1024]{1,0:T(8,128)(2,1)S(1)} %get-tuple-element.26), channel_id=1, source_target_pairs={{0,2},{1,3},{2,0},{3,1},{4,6},{5,7},{6,4},{7,5},{8,10},{9,11},{10,... | collective-permute-start | bytes 196616 | tf_op jit(solution)/shard_map/ppermute | solution.py:18
  25.5 4.9 %collective-permute-start.11 = (bf16[32,1024]{1,0:T(8,128)(2,1)S(1)}, bf16[32,1024]{1,0:T(8,128)(2,1)S(1)}, u32[]{:S(2)}, u32[]{:S(2)}) collective-permute-start(bf16[32,1024]{1,0:T(8,128)(2,1)S(1)} %add_convert_fusion.refs_0_), channel_id=1, source_target_pairs={{0,3},{1,0},{2,1},{3,2},{4,7},{5,4},{6,5},{7,6},{8,11},{9,8},{10,9... | collective-permute-start | bytes 196616 | tf_op jit(solution)/shard_map/ppermute | solution.py:18
  27.9 6.8 %collective-permute-start.10 = (bf16[32,1024]{1,0:T(8,128)(2,1)S(1)}, bf16[32,1024]{1,0:T(8,128)(2,1)S(1)}, u32[]{:S(2)}, u32[]{:S(2)}) collective-permute-start(bf16[32,1024]{1,0:T(8,128)(2,1)S(1)} %add_convert_fusion.refs_0_), channel_id=1, source_target_pairs={{0,2},{1,3},{2,0},{3,1},{4,6},{5,7},{6,4},{7,5},{8,10},{9,11},{10,... | collective-permute-start | bytes 196616 | tf_op jit(solution)/shard_map/ppermute | solution.py:18
  27.9 6.8 %collective-permute-start.9 = (bf16[32,1024]{1,0:T(8,128)(2,1)S(1)}, bf16[32,1024]{1,0:T(8,128)(2,1)S(1)}, u32[]{:S(2)}, u32[]{:S(2)}) collective-permute-start(bf16[32,1024]{1,0:T(8,128)(2,1)S(1)} %add_convert_fusion.refs_0_), channel_id=1, source_target_pairs={{0,1},{1,2},{2,3},{3,0},{4,5},{5,6},{6,7},{7,4},{8,9},{9,10},{10,1... | collective-permute-start | bytes 196616 | tf_op jit(solution)/shard_map/ppermute | solution.py:18

commit v3 on v2

--- a/solution.py
+++ b/solution.py
@@ -10,7 +10,7 @@
 RANGE = 3
 LANES = 128
 CODE_ROWS = 8
-OFFSETS = (0, 1, -1, 2, -2, 3, -3)
+OFFSETS = (0, 2, 3, -2, -3, 1, -1)
 
 
 def rotated(x, axis, by):
@@ -107,7 +107,7 @@
         out_shape=[pltpu.VMEM((rows, NTAB * KWIN), jnp.bfloat16)] * peers,
         name="bin",
     )(*map(near, arrived))
-    turns = sorted(range(1, peers), key=lambda r: (min(r, peers - r), r))
+    turns = list(range(1, peers))
     shares = [pieces[0]] + [rotated(pieces[r], "det", r) for r in turns]
     total = shares[0].astype(jnp.float32)
     for share in shares[1:]:

time: 35.8 us -> 33.9 us (0.947)
  waiting for transfers between devices: 15.6 us -> 12.8 us
  starting transfers between devices: 16.1 us -> 16.9 us
    ppermute x12, waiting for transfers between devices: 15.6 us -> 12.8 us  [rotated(): return lax.ppermute(x, axis, [(i, (i + by) % peers) for i in range(peers)])]
    ppermute x12, starting transfers between devices: 16.1 us -> 16.9 us  [rotated(): return lax.ppermute(x, axis, [(i, (i + by) % peers) for i in range(peers)])]
  transfers between devices with their start and end apart: 12 -> 12, of which waited for: 8 -> 9; matrix products, arithmetic and copies ran while one was open for 0% -> 0% of each run, Pallas kernels for 0% -> 0%
where the time goes in v3:
time: 33.9 us; the launch traced here: 33.8 us
  starting transfers between devices  16.9 us (50%)
  waiting for transfers between devices  12.8 us (38%)
  Pallas kernels  4.01 us (12%)
    ppermute x12, starting transfers between devices, rotated(): return lax.ppermute(x, axis, [(i, (i + by) % peers) for i in range(peers)])  16.9 us
    ppermute x12, waiting for transfers between devices, rotated(): return lax.ppermute(x, axis, [(i, (i + by) % peers) for i in range(peers)])  12.8 us
    pallas_call x1, Pallas kernels, body(): pl.pallas_call(cut_kernel, in_specs=[SMEM, SMEM, SMEM, ANY], out_specs=[V...  2.63 us
    pallas_call x1, Pallas kernels, body(): pl.pallas_call(image_kernel, in_specs=[VMEM] * (peers + 1), out_specs=VME...  1.04 us
  transfers between devices with their start and end apart: 12, of which 9 were waited for; matrix products, arithmetic and copies ran while one was open for 0% of the time, Pallas kernels for 0%

profile of v3, /device:TPU:0, one launch (start us, length us, event | category | flops | bytes accessed | tf_op | source)
XLA Modules:
  0.0 33.8 jit_solution(2510208197051209203)
XLA Ops:
  0.0 2.6 %cut.1 = (bf16[136,256]{1,0:T(8,128)(2,1)S(1)}, bf16[136,256]{1,0:T(8,128)(2,1)S(1)}, bf16[136,256]{1,0:T(8,128)(2,1)S(1)}, bf16[136,256]{1,0:T(8,128)(2,1)S(1)}...) custom-call(s32[1,7]{1,0:T(1,128)} %starts.1, s32[1,7]{1,0:T(1,128)} %slots.1, ...), custom_call_target="tpu_custom_call" | custom-call | tf_op jit(solution)/shard_map/cut/pallas_call | solution.py:91
  2.6 3.0 %collective-permute-start = (bf16[136,256]{1,0:T(8,128)(2,1)S(1)}, bf16[136,256]{1,0:T(8,128)(2,1)S(1)}, u32[]{:S(2)}, u32[]{:S(2)}) collective-permute-start(bf16[136,256]{1,0:T(8,128)(2,1)S(1)} %get-tuple-element.17), channel_id=1, source_target_pairs={{0,8},{4,12},{8,16},{12,20},{16,24},{20,28},{24,0},{28,4},{1,9},{5... | collective-permute-start | bytes 208904 | tf_op jit(solution)/shard_map/ppermute | solution.py:18
  5.7 0.7 %collective-permute-start.1 = (bf16[136,256]{1,0:T(8,128)(2,1)S(1)}, bf16[136,256]{1,0:T(8,128)(2,1)S(1)}, u32[]{:S(2)}, u32[]{:S(2)}) collective-permute-start(bf16[136,256]{1,0:T(8,128)(2,1)S(1)} %get-tuple-element.18), channel_id=1, source_target_pairs={{0,12},{4,16},{8,20},{12,24},{16,28},{20,0},{24,4},{28,8},{1,13},{... | collective-permute-start | bytes 208904 | tf_op jit(solution)/shard_map/ppermute | solution.py:18
  6.3 1.4 %collective-permute-start.2 = (bf16[136,256]{1,0:T(8,128)(2,1)S(1)}, bf16[136,256]{1,0:T(8,128)(2,1)S(1)}, u32[]{:S(2)}, u32[]{:S(2)}) collective-permute-start(bf16[136,256]{1,0:T(8,128)(2,1)S(1)} %get-tuple-element.19), channel_id=1, source_target_pairs={{0,24},{4,28},{8,0},{12,4},{16,8},{20,12},{24,16},{28,20},{1,25},{... | collective-permute-start | bytes 208904 | tf_op jit(solution)/shard_map/ppermute | solution.py:18
  7.7 0.4 %collective-permute-start.3 = (bf16[136,256]{1,0:T(8,128)(2,1)S(1)}, bf16[136,256]{1,0:T(8,128)(2,1)S(1)}, u32[]{:S(2)}, u32[]{:S(2)}) collective-permute-start(bf16[136,256]{1,0:T(8,128)(2,1)S(1)} %get-tuple-element.20), channel_id=1, source_target_pairs={{0,20},{4,24},{8,28},{12,0},{16,4},{20,8},{24,12},{28,16},{1,21},{... | collective-permute-start | bytes 208904 | tf_op jit(solution)/shard_map/ppermute | solution.py:18
  8.1 0.6 %collective-permute-start.4 = (bf16[136,256]{1,0:T(8,128)(2,1)S(1)}, bf16[136,256]{1,0:T(8,128)(2,1)S(1)}, u32[]{:S(2)}, u32[]{:S(2)}) collective-permute-start(bf16[136,256]{1,0:T(8,128)(2,1)S(1)} %get-tuple-element.21), channel_id=1, source_target_pairs={{0,4},{4,8},{8,12},{12,16},{16,20},{20,24},{24,28},{28,0},{1,5},{5... | collective-permute-start | bytes 208904 | tf_op jit(solution)/shard_map/ppermute | solution.py:18
  8.8 0.2 collective-permute-done.refs_1_
  8.9 1.9 %collective-permute-start.5 = (bf16[136,256]{1,0:T(8,128)(2,1)S(1)}, bf16[136,256]{1,0:T(8,128)(2,1)S(1)}, u32[]{:S(2)}, u32[]{:S(2)}) collective-permute-start(bf16[136,256]{1,0:T(8,128)(2,1)S(1)} %get-tuple-element.22), channel_id=1, source_target_pairs={{0,28},{4,0},{8,4},{12,8},{16,12},{20,16},{24,20},{28,24},{1,29},{... | collective-permute-start | bytes 208904 | tf_op jit(solution)/shard_map/ppermute | solution.py:18
  10.8 1.2 %collective-permute-done.2.refs_3_ = bf16[136,256]{1,0:T(8,128)(2,1)S(1)} collective-permute-done((bf16[136,256]{1,0:T(8,128)(2,1)S(1)}, bf16[136,256]{1,0:T(8,128)(2,1)S(1)}, u32[]{:S(2)}, u32[]{:S(2)}) %collective-permute-start.2) | collective-permute-done | bytes 69664 | tf_op jit(solution)/shard_map/ppermute | solution.py:18
  12.0 0.5 %collective-permute-done.3.refs_4_ = bf16[136,256]{1,0:T(8,128)(2,1)S(1)} collective-permute-done((bf16[136,256]{1,0:T(8,128)(2,1)S(1)}, bf16[136,256]{1,0:T(8,128)(2,1)S(1)}, u32[]{:S(2)}, u32[]{:S(2)}) %collective-permute-start.3) | collective-permute-done | bytes 69664 | tf_op jit(solution)/shard_map/ppermute | solution.py:18
  12.4 0.8 %collective-permute-done.4.refs_5_ = bf16[136,256]{1,0:T(8,128)(2,1)S(1)} collective-permute-done((bf16[136,256]{1,0:T(8,128)(2,1)S(1)}, bf16[136,256]{1,0:T(8,128)(2,1)S(1)}, u32[]{:S(2)}, u32[]{:S(2)}) %collective-permute-start.4) | collective-permute-done | bytes 69664 | tf_op jit(solution)/shard_map/ppermute | solution.py:18
  13.2 0.3 %bin.1 = (bf16[32,1024]{1,0:T(8,128)(2,1)S(1)}, bf16[32,1024]{1,0:T(8,128)(2,1)S(1)}, bf16[32,1024]{1,0:T(8,128)(2,1)S(1)}, bf16[32,1024]{1,0:T(8,128)(2,1)S(1)}) custom-call(bf16[136,256]{1,0:T(8,128)(2,1)S(1)} %get-tuple-element.16.refs_0_, bf16[136,256]{1,0:T(8,128)(2,1)S(1)} %collective-permute-done.refs_1_, ...), custom_call_target="tpu_custom_call" | custom-call | tf_op jit(solution)/shard_map/bin/pallas_call | solution.py:103
  13.5 1.6 %collective-permute-start.6 = (bf16[32,1024]{1,0:T(8,128)(2,1)S(1)}, bf16[32,1024]{1,0:T(8,128)(2,1)S(1)}, u32[]{:S(2)}, u32[]{:S(2)}) collective-permute-start(bf16[32,1024]{1,0:T(8,128)(2,1)S(1)} %get-tuple-element.24), channel_id=1, source_target_pairs={{0,1},{1,2},{2,3},{3,0},{4,5},{5,6},{6,7},{7,4},{8,9},{9,10},{10,1... | collective-permute-start | bytes 196616 | tf_op jit(solution)/shard_map/ppermute | solution.py:18
  15.2 2.7 %collective-permute-start.7 = (bf16[32,1024]{1,0:T(8,128)(2,1)S(1)}, bf16[32,1024]{1,0:T(8,128)(2,1)S(1)}, u32[]{:S(2)}, u32[]{:S(2)}) collective-permute-start(bf16[32,1024]{1,0:T(8,128)(2,1)S(1)} %get-tuple-element.25), channel_id=1, source_target_pairs={{0,2},{1,3},{2,0},{3,1},{4,6},{5,7},{6,4},{7,5},{8,10},{9,11},{10,... | collective-permute-start | bytes 196616 | tf_op jit(solution)/shard_map/ppermute | solution.py:18
  17.8 1.3 %collective-permute-start.8 = (bf16[32,1024]{1,0:T(8,128)(2,1)S(1)}, bf16[32,1024]{1,0:T(8,128)(2,1)S(1)}, u32[]{:S(2)}, u32[]{:S(2)}) collective-permute-start(bf16[32,1024]{1,0:T(8,128)(2,1)S(1)} %get-tuple-element.26), channel_id=1, source_target_pairs={{0,3},{1,0},{2,1},{3,2},{4,7},{5,4},{6,5},{7,6},{8,11},{9,8},{10,9... | collective-permute-start | bytes 196616 | tf_op jit(solution)/shard_map/ppermute | solution.py:18
  19.1 1.0 %collective-permute-done.6 = bf16[32,1024]{1,0:T(8,128)(2,1)S(1)} collective-permute-done((bf16[32,1024]{1,0:T(8,128)(2,1)S(1)}, bf16[32,1024]{1,0:T(8,128)(2,1)S(1)}, u32[]{:S(2)}, u32[]{:S(2)}) %collective-permute-start.6) | collective-permute-done | bytes 65568 | tf_op jit(solution)/shard_map/ppermute | solution.py:18
  20.1 2.8 %collective-permute-done.7 = bf16[32,1024]{1,0:T(8,128)(2,1)S(1)} collective-permute-done((bf16[32,1024]{1,0:T(8,128)(2,1)S(1)}, bf16[32,1024]{1,0:T(8,128)(2,1)S(1)}, u32[]{:S(2)}, u32[]{:S(2)}) %collective-permute-start.7) | collective-permute-done | bytes 65568 | tf_op jit(solution)/shard_map/ppermute | solution.py:18
  22.9 0.3 collective-permute-done.8
  23.2 2.7 %collective-permute-start.11 = (bf16[32,1024]{1,0:T(8,128)(2,1)S(1)}, bf16[32,1024]{1,0:T(8,128)(2,1)S(1)}, u32[]{:S(2)}, u32[]{:S(2)}) collective-permute-start(bf16[32,1024]{1,0:T(8,128)(2,1)S(1)} %add_convert_fusion.refs_0_), channel_id=1, source_target_pairs={{0,3},{1,0},{2,1},{3,2},{4,7},{5,4},{6,5},{7,6},{8,11},{9,8},{10,9... | collective-permute-start | bytes 196616 | tf_op jit(solution)/shard_map/ppermute | solution.py:18
  25.9 0.4 %collective-permute-start.10 = (bf16[32,1024]{1,0:T(8,128)(2,1)S(1)}, bf16[32,1024]{1,0:T(8,128)(2,1)S(1)}, u32[]{:S(2)}, u32[]{:S(2)}) collective-permute-start(bf16[32,1024]{1,0:T(8,128)(2,1)S(1)} %add_convert_fusion.refs_0_), channel_id=1, source_target_pairs={{0,2},{1,3},{2,0},{3,1},{4,6},{5,7},{6,4},{7,5},{8,10},{9,11},{10,... | collective-permute-start | bytes 196616 | tf_op jit(solution)/shard_map/ppermute | solution.py:18
  26.3 0.2 collective-permute-start.9
  26.5 1.8 %collective-permute-done.11.refs_3_ = bf16[32,1024]{1,0:T(8,128)(2,1)S(1)} collective-permute-done((bf16[32,1024]{1,0:T(8,128)(2,1)S(1)}, bf16[32,1024]{1,0:T(8,128)(2,1)S(1)}, u32[]{:S(2)}, u32[]{:S(2)}) %collective-permute-start.11) | collective-permute-done | bytes 65568 | tf_op jit(solution)/shard_map/ppermute | solution.py:18
  28.4 4.4 %collective-permute-done.10.refs_2_ = bf16[32,1024]{1,0:T(8,128)(2,1)S(1)} collective-permute-done((bf16[32,1024]{1,0:T(8,128)(2,1)S(1)}, bf16[32,1024]{1,0:T(8,128)(2,1)S(1)}, u32[]{:S(2)}, u32[]{:S(2)}) %collective-permute-start.10) | collective-permute-done | bytes 65568 | tf_op jit(solution)/shard_map/ppermute | solution.py:18
  32.7 1.0 %image.1 = f32[128,512]{1,0:T(8,128)} custom-call(bf16[32,1024]{1,0:T(8,128)(2,1)S(1)} %add_convert_fusion.refs_0_, bf16[32,1024]{1,0:T(8,128)(2,1)S(1)} %collective-permute-done.9.refs_1_, bf16[32,1024]{1,0:T(8,128)(2,1)S(1)} %collective-permute-done.10.refs_2_, bf16[32,1024]{1,0:T(8,128)(2,1)S(1)} %collective-permute-done.11.refs_3_, ...), custom_call_target="tpu_custom_call" | custom-call | tf_op jit(solution)/shard_map/image/pallas_call | solution.py:118
  (6 shorter events, 0.0 us)
Async XLA Ops:
  0.0 32.7 %copy-start = (bf16[4,256,512]{2,1,0:T(8,128)(2,1)S(1)}, bf16[4,256,512]{2,1,0:T(8,128)(2,1)}, u32[]{:S(2)}) copy-start(bf16[4,256,512]{2,1,0:T(8,128)(2,1)} %refs_4_.1) | copy-start | bytes 3145732
  2.6 6.3 %collective-permute-start = (bf16[136,256]{1,0:T(8,128)(2,1)S(1)}, bf16[136,256]{1,0:T(8,128)(2,1)S(1)}, u32[]{:S(2)}, u32[]{:S(2)}) collective-permute-start(bf16[136,256]{1,0:T(8,128)(2,1)S(1)} %get-tuple-element.17), channel_id=1, source_target_pairs={{0,8},{4,12},{8,16},{12,20},{16,24},{20,28},{24,0},{28,4},{1,9},{5... | collective-permute-start | bytes 208904 | tf_op jit(solution)/shard_map/ppermute | solution.py:18
  5.7 5.1 %collective-permute-start.1 = (bf16[136,256]{1,0:T(8,128)(2,1)S(1)}, bf16[136,256]{1,0:T(8,128)(2,1)S(1)}, u32[]{:S(2)}, u32[]{:S(2)}) collective-permute-start(bf16[136,256]{1,0:T(8,128)(2,1)S(1)} %get-tuple-element.18), channel_id=1, source_target_pairs={{0,12},{4,16},{8,20},{12,24},{16,28},{20,0},{24,4},{28,8},{1,13},{... | collective-permute-start | bytes 208904 | tf_op jit(solution)/shard_map/ppermute | solution.py:18
  6.3 5.7 %collective-permute-start.2 = (bf16[136,256]{1,0:T(8,128)(2,1)S(1)}, bf16[136,256]{1,0:T(8,128)(2,1)S(1)}, u32[]{:S(2)}, u32[]{:S(2)}) collective-permute-start(bf16[136,256]{1,0:T(8,128)(2,1)S(1)} %get-tuple-element.19), channel_id=1, source_target_pairs={{0,24},{4,28},{8,0},{12,4},{16,8},{20,12},{24,16},{28,20},{1,25},{... | collective-permute-start | bytes 208904 | tf_op jit(solution)/shard_map/ppermute | solution.py:18
  7.7 4.7 %collective-permute-start.3 = (bf16[136,256]{1,0:T(8,128)(2,1)S(1)}, bf16[136,256]{1,0:T(8,128)(2,1)S(1)}, u32[]{:S(2)}, u32[]{:S(2)}) collective-permute-start(bf16[136,256]{1,0:T(8,128)(2,1)S(1)} %get-tuple-element.20), channel_id=1, source_target_pairs={{0,20},{4,24},{8,28},{12,0},{16,4},{20,8},{24,12},{28,16},{1,21},{... | collective-permute-start | bytes 208904 | tf_op jit(solution)/shard_map/ppermute | solution.py:18
  8.1 5.0 %collective-permute-start.4 = (bf16[136,256]{1,0:T(8,128)(2,1)S(1)}, bf16[136,256]{1,0:T(8,128)(2,1)S(1)}, u32[]{:S(2)}, u32[]{:S(2)}) collective-permute-start(bf16[136,256]{1,0:T(8,128)(2,1)S(1)} %get-tuple-element.21), channel_id=1, source_target_pairs={{0,4},{4,8},{8,12},{12,16},{16,20},{20,24},{24,28},{28,0},{1,5},{5... | collective-permute-start | bytes 208904 | tf_op jit(solution)/shard_map/ppermute | solution.py:18
  8.9 4.3 %collective-permute-start.5 = (bf16[136,256]{1,0:T(8,128)(2,1)S(1)}, bf16[136,256]{1,0:T(8,128)(2,1)S(1)}, u32[]{:S(2)}, u32[]{:S(2)}) collective-permute-start(bf16[136,256]{1,0:T(8,128)(2,1)S(1)} %get-tuple-element.22), channel_id=1, source_target_pairs={{0,28},{4,0},{8,4},{12,8},{16,12},{20,16},{24,20},{28,24},{1,29},{... | collective-permute-start | bytes 208904 | tf_op jit(solution)/shard_map/ppermute | solution.py:18
  13.5 6.6 %collective-permute-start.6 = (bf16[32,1024]{1,0:T(8,128)(2,1)S(1)}, bf16[32,1024]{1,0:T(8,128)(2,1)S(1)}, u32[]{:S(2)}, u32[]{:S(2)}) collective-permute-start(bf16[32,1024]{1,0:T(8,128)(2,1)S(1)} %get-tuple-element.24), channel_id=1, source_target_pairs={{0,1},{1,2},{2,3},{3,0},{4,5},{5,6},{6,7},{7,4},{8,9},{9,10},{10,1... | collective-permute-start | bytes 196616 | tf_op jit(solution)/shard_map/ppermute | solution.py:18
  15.2 7.7 %collective-permute-start.7 = (bf16[32,1024]{1,0:T(8,128)(2,1)S(1)}, bf16[32,1024]{1,0:T(8,128)(2,1)S(1)}, u32[]{:S(2)}, u32[]{:S(2)}) collective-permute-start(bf16[32,1024]{1,0:T(8,128)(2,1)S(1)} %get-tuple-element.25), channel_id=1, source_target_pairs={{0,2},{1,3},{2,0},{3,1},{4,6},{5,7},{6,4},{7,5},{8,10},{9,11},{10,... | collective-permute-start | bytes 196616 | tf_op jit(solution)/shard_map/ppermute | solution.py:18
  17.8 5.3 %collective-permute-start.8 = (bf16[32,1024]{1,0:T(8,128)(2,1)S(1)}, bf16[32,1024]{1,0:T(8,128)(2,1)S(1)}, u32[]{:S(2)}, u32[]{:S(2)}) collective-permute-start(bf16[32,1024]{1,0:T(8,128)(2,1)S(1)} %get-tuple-element.26), channel_id=1, source_target_pairs={{0,3},{1,0},{2,1},{3,2},{4,7},{5,4},{6,5},{7,6},{8,11},{9,8},{10,9... | collective-permute-start | bytes 196616 | tf_op jit(solution)/shard_map/ppermute | solution.py:18
  23.2 5.2 %collective-permute-start.11 = (bf16[32,1024]{1,0:T(8,128)(2,1)S(1)}, bf16[32,1024]{1,0:T(8,128)(2,1)S(1)}, u32[]{:S(2)}, u32[]{:S(2)}) collective-permute-start(bf16[32,1024]{1,0:T(8,128)(2,1)S(1)} %add_convert_fusion.refs_0_), channel_id=1, source_target_pairs={{0,3},{1,0},{2,1},{3,2},{4,7},{5,4},{6,5},{7,6},{8,11},{9,8},{10,9... | collective-permute-start | bytes 196616 | tf_op jit(solution)/shard_map/ppermute | solution.py:18
  25.9 6.8 %collective-permute-start.10 = (bf16[32,1024]{1,0:T(8,128)(2,1)S(1)}, bf16[32,1024]{1,0:T(8,128)(2,1)S(1)}, u32[]{:S(2)}, u32[]{:S(2)}) collective-permute-start(bf16[32,1024]{1,0:T(8,128)(2,1)S(1)} %add_convert_fusion.refs_0_), channel_id=1, source_target_pairs={{0,2},{1,3},{2,0},{3,1},{4,6},{5,7},{6,4},{7,5},{8,10},{9,11},{10,... | collective-permute-start | bytes 196616 | tf_op jit(solution)/shard_map/ppermute | solution.py:18
  26.3 6.5 %collective-permute-start.9 = (bf16[32,1024]{1,0:T(8,128)(2,1)S(1)}, bf16[32,1024]{1,0:T(8,128)(2,1)S(1)}, u32[]{:S(2)}, u32[]{:S(2)}) collective-permute-start(bf16[32,1024]{1,0:T(8,128)(2,1)S(1)} %add_convert_fusion.refs_0_), channel_id=1, source_target_pairs={{0,1},{1,2},{2,3},{3,0},{4,5},{5,6},{6,7},{7,4},{8,9},{9,10},{10,1... | collective-permute-start | bytes 196616 | tf_op jit(solution)/shard_map/ppermute | solution.py:18
